TPU v7x, 32 devices: a whole 2x2x4 slice. The times are simulated.
32 devices in a mesh: tp: 8 (over z, y), cp: 4 (over x, core).
Axes of the slice: x: 2, y: 2, z: 4, core: 2. Of those that a mesh axis runs over, the one named last changes fastest.
Arguments:
- tokens: int32 [4096], P('cp')
- pos: int32 [4096], P('cp')
- doc_id: int32 [4096], P('cp')
- dy: bfloat16 [4096, 2048], P('cp')
- table: bfloat16 [32256, 2048], P('tp')
- w_q: bfloat16 [2048, 2048], P(None, 'tp')
- w_k: bfloat16 [2048, 2048], P(None, 'tp')
- w_v: bfloat16 [2048, 2048], P(None, 'tp')
- w_o: bfloat16 [2048, 2048], P('tp')
- w_gate: bfloat16 [2048, 5504], P(None, 'tp')
- w_up: bfloat16 [2048, 5504], P(None, 'tp')
- w_down: bfloat16 [5504, 2048], P('tp')
- gain_one: bfloat16 [2048], replicated
- gain_two: bfloat16 [2048], replicated
- inv_freq: float32 [64], replicated
Outputs:
- output 1: bfloat16 [4096, 2048], P('cp')
- output 2: float32 [32256, 2048], P('tp')
- output 3: float32 [2048, 2048], P(None, 'tp')
- output 4: float32 [2048, 2048], P(None, 'tp')
- output 5: float32 [2048, 2048], P(None, 'tp')
- output 6: float32 [2048, 2048], P('tp')
- output 7: float32 [2048, 5504], P(None, 'tp')
- output 8: float32 [2048, 5504], P(None, 'tp')
- output 9: float32 [5504, 2048], P('tp')
- output 10: float32 [2048], replicated
- output 11: float32 [2048], replicated
All inputs are finite; a program needn't handle non-finite values.
Results may differ from a plain program's by a relative error of at most 0.0147249.
Values are sent between devices in bfloat16 or wider.
A program may use at most 1 GiB of HBM per device.

v0:
```python
import jax
import jax.numpy as jnp
from jax import lax
from jax.sharding import PartitionSpec as P

NORM_EPS = 1e-5
NEG_BIG = -1e30


def rms_stats(feats):
    inv_rms = lax.rsqrt(jnp.mean(feats * feats, axis=-1, keepdims=True) + NORM_EPS)
    return feats * inv_rms, inv_rms


def rms_back(d_normed, normed, inv_rms):
    return inv_rms * (d_normed - normed * jnp.mean(d_normed * normed, axis=-1, keepdims=True))


def rotate(tensor_in, cosine, sine):
    half = tensor_in.shape[-1] // 2
    first = tensor_in[..., :half]
    second = tensor_in[..., half:]
    return jnp.concatenate([first * cosine - second * sine, second * cosine + first * sine], axis=-1)


def to_bf16(feats):
    return feats.astype(jnp.bfloat16).astype(jnp.float32)


def slot_sequence(slot, block_len, cp_count):
    shard = slot // (2 * block_len)
    within = slot % (2 * block_len)
    block_no = jnp.where(within < block_len, shard, 2 * cp_count - 1 - shard)
    return block_no * block_len + within % block_len


def solution(mesh):
    cp_count = mesh.shape["cp"]

    def device_step(tokens, pos, doc_id, dy, table, w_q, w_k, w_v, w_o, w_gate, w_up, w_down, gain_one, gain_two, inv_freq):
        span = tokens.shape[0]
        total = span * cp_count
        rows = table.shape[0]
        head_dim = 2 * inv_freq.shape[0]
        kv_local = w_k.shape[1] // head_dim
        q_local = w_q.shape[1] // head_dim
        group = q_local // kv_local
        scale = head_dim ** -0.5
        tp_rank = lax.axis_index("tp")
        cp_rank = lax.axis_index("cp")
        gain_a = gain_one.astype(jnp.float32)
        gain_b = gain_two.astype(jnp.float32)

        local_ids = tokens - tp_rank * rows
        owned = (local_ids >= 0) & (local_ids < rows)
        safe_ids = jnp.where(owned, local_ids, 0)
        picked = jnp.where(owned[:, None], jnp.take(table, safe_ids, axis=0), jnp.zeros((), jnp.bfloat16))
        embed = lax.psum(picked, "tp").astype(jnp.float32)

        normed_a, inv_a = rms_stats(embed)
        act_a = (normed_a * gain_a).astype(jnp.bfloat16)
        angle = pos.astype(jnp.float32)[:, None, None] * inv_freq
        cosine = jnp.cos(angle)
        sine = jnp.sin(angle)
        query = jnp.dot(act_a, w_q, preferred_element_type=jnp.float32).reshape(span, q_local, head_dim)
        query = rotate(query, cosine, sine).astype(jnp.bfloat16).reshape(span, kv_local, group, head_dim)
        key_loc = jnp.dot(act_a, w_k, preferred_element_type=jnp.float32).reshape(span, kv_local, head_dim)
        key_loc = rotate(key_loc, cosine, sine).astype(jnp.bfloat16)
        value_loc = jnp.dot(act_a, w_v, preferred_element_type=jnp.float32).astype(jnp.bfloat16).reshape(span, kv_local, head_dim)

        key_all = lax.all_gather(key_loc, "cp", axis=0, tiled=True)
        value_all = lax.all_gather(value_loc, "cp", axis=0, tiled=True)
        doc_all = lax.all_gather(doc_id, "cp", axis=0, tiled=True)
        q_seq = slot_sequence(cp_rank * span + jnp.arange(span), span // 2, cp_count)
        k_seq = slot_sequence(jnp.arange(total), span // 2, cp_count)
        allowed = (doc_id[:, None] == doc_all[None, :]) & (k_seq[None, :] <= q_seq[:, None])

        scores = jnp.einsum("qkgd,skd->kgqs", query, key_all, preferred_element_type=jnp.float32) * scale
        attn_prob = jax.nn.softmax(jnp.where(allowed, scores, NEG_BIG), axis=-1)
        prob_b = attn_prob.astype(jnp.bfloat16)
        attended = jnp.einsum("kgqs,skd->qkgd", prob_b, value_all, preferred_element_type=jnp.float32)
        attended = attended.astype(jnp.bfloat16).reshape(span, q_local * head_dim)
        residual = embed + lax.psum(jnp.dot(attended, w_o, preferred_element_type=jnp.float32), "tp")
        normed_b, inv_b = rms_stats(residual)
        act_b = (normed_b * gain_b).astype(jnp.bfloat16)
        gate = jnp.dot(act_b, w_gate, preferred_element_type=jnp.float32)
        up_val = jnp.dot(act_b, w_up, preferred_element_type=jnp.float32)
        gate_sig = jax.nn.sigmoid(gate)
        hidden = (gate * gate_sig * up_val).astype(jnp.bfloat16)
        layer_out = residual + lax.psum(jnp.dot(hidden, w_down, preferred_element_type=jnp.float32), "tp")

        grad_down = jnp.einsum("tf,td->fd", hidden, dy, preferred_element_type=jnp.float32)
        d_hidden = to_bf16(jnp.einsum("td,fd->tf", dy, w_down, preferred_element_type=jnp.float32))
        d_gate = (d_hidden * up_val * gate_sig * (1.0 + gate * (1.0 - gate_sig))).astype(jnp.bfloat16)
        d_up = (d_hidden * gate * gate_sig).astype(jnp.bfloat16)
        grad_gate = jnp.einsum("td,tf->df", act_b, d_gate, preferred_element_type=jnp.float32)
        grad_up = jnp.einsum("td,tf->df", act_b, d_up, preferred_element_type=jnp.float32)
        d_act_b = jnp.einsum("tf,df->td", d_gate, w_gate, preferred_element_type=jnp.float32)
        d_act_b = d_act_b + jnp.einsum("tf,df->td", d_up, w_up, preferred_element_type=jnp.float32)
        d_act_b = to_bf16(lax.psum(d_act_b, "tp"))
        grad_gain_b = jnp.sum(d_act_b * normed_b, axis=0)
        d_resid = dy.astype(jnp.float32) + rms_back(d_act_b * gain_b, normed_b, inv_b)
        d_resid_b = d_resid.astype(jnp.bfloat16)
        grad_out = jnp.einsum("tc,td->cd", attended, d_resid_b, preferred_element_type=jnp.float32)
        d_att = jnp.einsum("td,cd->tc", d_resid_b, w_o, preferred_element_type=jnp.float32)
        d_att = d_att.astype(jnp.bfloat16).reshape(span, kv_local, group, head_dim)
        d_prob = to_bf16(jnp.einsum("qkgd,skd->kgqs", d_att, value_all, preferred_element_type=jnp.float32))
        d_scores = attn_prob * (d_prob - jnp.sum(attn_prob * d_prob, axis=-1, keepdims=True))
        d_scores = (d_scores * scale).astype(jnp.bfloat16)
        d_query = jnp.einsum("kgqs,skd->qkgd", d_scores, key_all, preferred_element_type=jnp.float32)
        d_key_all = jnp.einsum("kgqs,qkgd->skd", d_scores, query, preferred_element_type=jnp.float32)
        d_value_all = jnp.einsum("kgqs,qkgd->skd", prob_b, d_att, preferred_element_type=jnp.float32)
        d_key = lax.psum_scatter(d_key_all, "cp", scatter_dimension=0, tiled=True)
        d_value = lax.psum_scatter(d_value_all, "cp", scatter_dimension=0, tiled=True)
        d_q_pre = rotate(to_bf16(d_query).reshape(span, q_local, head_dim), cosine, -sine)
        d_q_pre = d_q_pre.astype(jnp.bfloat16).reshape(span, q_local * head_dim)
        d_k_pre = rotate(to_bf16(d_key), cosine, -sine).astype(jnp.bfloat16).reshape(span, kv_local * head_dim)
        d_v_pre = d_value.astype(jnp.bfloat16).reshape(span, kv_local * head_dim)
        grad_q = jnp.einsum("td,tc->dc", act_a, d_q_pre, preferred_element_type=jnp.float32)
        grad_k = jnp.einsum("td,tc->dc", act_a, d_k_pre, preferred_element_type=jnp.float32)
        grad_v = jnp.einsum("td,tc->dc", act_a, d_v_pre, preferred_element_type=jnp.float32)
        d_act_a = jnp.einsum("tc,dc->td", d_q_pre, w_q, preferred_element_type=jnp.float32)
        d_act_a = d_act_a + jnp.einsum("tc,dc->td", d_k_pre, w_k, preferred_element_type=jnp.float32)
        d_act_a = d_act_a + jnp.einsum("tc,dc->td", d_v_pre, w_v, preferred_element_type=jnp.float32)
        d_act_a = to_bf16(lax.psum(d_act_a, "tp"))
        grad_gain_a = jnp.sum(d_act_a * normed_a, axis=0)
        d_embed = d_resid + rms_back(d_act_a * gain_a, normed_a, inv_a)
        table_part = jax.ops.segment_sum(jnp.where(owned[:, None], d_embed, 0.0), safe_ids, num_segments=rows)
        grad_table = lax.psum(table_part, "cp")
        weight_grads = lax.psum((grad_q, grad_k, grad_v, grad_out, grad_gate, grad_up, grad_down, grad_gain_a, grad_gain_b), "cp")
        return (layer_out.astype(jnp.bfloat16), grad_table) + tuple(weight_grads)

    col_spec = P(None, "tp")
    row_spec = P("tp", None)
    tok_spec = P("cp")
    rep_spec = P(None)
    in_specs = (tok_spec, tok_spec, tok_spec, P("cp", None), row_spec, col_spec, col_spec, col_spec, row_spec, col_spec, col_spec, row_spec, rep_spec, rep_spec, rep_spec)
    out_specs = (P("cp", None), row_spec, col_spec, col_spec, col_spec, row_spec, col_spec, col_spec, row_spec, rep_spec, rep_spec)
    return jax.shard_map(device_step, mesh=mesh, in_specs=in_specs, out_specs=out_specs, check_vma=False)
```

profile of v0, /device:TPU:0, one launch (start us, length us, event | category | flops | bytes accessed | tf_op | source)
XLA Modules:
  0.0 2588.4 jit_solution(18158042347144067673)
XLA Ops:
  8.7 16.6 gather_fusion
  33.2 154.4 %all-reduce.9.cloned.1.call-done = bf16[1024,2048]{1,0:T(8,128)(2,1)} async-done(((bf16[1024,2048]{1,0:T(8,128)(2,1)}), bf16[1024,2048]{1,0:T(8,128)(2,1)}) %all-reduce.9.cloned.1.call-update) | async-done | bytes 4194320 | tf_op jit(solution)/shard_map/psum | solution.py:58
  214.6 5.5 all_gather.10
  229.1 7.0 all-gather.5.cloned.1.call-done
  236.1 16.7 fusion.8
  252.9 15.0 fusion.7
  267.9 17.8 fusion.50
  285.7 6.1 fusion.89
  292.5 7.3 convolution_convert_fusion.1
  299.8 260.7 %all-reduce.11.cloned.1.call-done = f32[1024,2048]{1,0:T(8,128)} async-done(((f32[1024,2048]{1,0:T(8,128)}), f32[1024,2048]{1,0:T(8,128)}) %all-reduce.11.cloned.1.call-update) | async-done | bytes 8388624 | tf_op jit(solution)/shard_map/psum | solution.py:83
  560.5 5.7 multiply_reduce_fusion
  579.6 5.7 fusion.91
  585.6 5.9 fusion.92
  591.5 6.1 convolution_add_fusion
  597.7 393.8 %all-reduce.16 = bf16[1024,2048]{1,0:T(8,128)(2,1)} all-reduce(f32[1024,2048]{1,0:T(8,128)} %convolution_add_fusion), channel_id=1, replica_groups=mesh['tp'=8,'cp'=4] {'tp'}, use_global_device_ids=true, to_apply=%region_7.8 | all-reduce | flops 2097152 | bytes 12582912 | tf_op jit(solution)/shard_map/psum | solution.py:100
  991.4 6.5 fusion.30
  998.0 36.6 %all-reduce.13.cloned.1.call-done = f32[1024,2048]{1,0:T(8,128)} async-done(((f32[1024,2048]{1,0:T(8,128)}), f32[1024,2048]{1,0:T(8,128)}) %all-reduce.13.cloned.1.call-update) | async-done | bytes 8388624 | tf_op jit(solution)/shard_map/psum | solution.py:90
  1034.6 12.4 fusion.29
  1050.3 22.1 fusion.2
  1072.4 26.5 %fusion.9 = bf16[2,1024,4096]{1,2,0:T(8,128)(2,1)} fusion(bf16[2,4096,1024]{2,1,0:T(8,128)(2,1)} %get-tuple-element.56, f32[2,1024]{1,0:T(2,128)S(1)} %get-tuple-element.55, f32[2,1024]{1,0:T(2,128)S(1)} %fusion.7, f32[2,1024]{1,0:T(2,128)S(1)} %get-tuple-element.53, f32[2,4096,1024]{2,1,0:T(8,128)} %get-tuple-element.54, pred[1024,4096]{0,1:T(8,128)(4,1)} %compare_and_fusion), kind=kLoop, calls=%fused_computation.14 | loop fusion | flops 75497472 | bytes 71327744 | tf_op jit(solution)/shard_map/reshape.22
  1098.9 10.6 convolution_bitcast_fusion
  1109.5 18.3 fusion.35
  1129.2 7.2 fusion.99
  1148.8 11.0 fusion.55
  1180.0 21.7 reduce-scatter.5.cloned.1.call-done
  1208.3 8.1 add_add_fusion
  1216.4 324.3 %all-reduce.17 = bf16[1024,2048]{1,0:T(8,128)(2,1)} all-reduce(f32[1024,2048]{1,0:T(8,128)} %add_add_fusion), channel_id=1, replica_groups=mesh['tp'=8,'cp'=4] {'tp'}, use_global_device_ids=true, to_apply=%region_12.13 | all-reduce | flops 2097152 | bytes 12582912 | tf_op jit(solution)/shard_map/psum | solution.py:125
  1546.6 7.1 fusion.26
  1553.8 28.5 %scatter_custom_fusion = f32[4032,2048]{1,0:T(8,128)} fusion(s32[1024]{0:T(1024)} %copy-done.36, f32[1024,2048]{1,0:T(8,128)} %fusion.26, f32[]{:T(128)} %constant.103.clone.1), kind=kCustom, calls=%fused_computation.20 | custom fusion | flops 2097152 | bytes 33030656 | tf_op jit(solution)/shard_map/scatter-add | solution.py:128
  1583.0 14.1 all-reduce
  1597.1 942.5 %all-reduce.15.cloned.1.call-done = (f32[4032,2048]{1,0:T(8,128)}, f32[2048,256]{1,0:T(8,128)}, f32[2048,256]{1,0:T(8,128)}, f32[2048,256]{1,0:T(8,128)}, f32[25...) async-done(((f32[4032,2048]{1,0:T(8,128)}, f32[2048,256]{1,0:T(8,128)}, f32[2048,256]{1,0:T(8,128)}, f32[2048,256]{1,0:T(8,128)}, ...) | async-done | bytes 58327056 | tf_op jit(solution)/shard_map/psum | solution.py:129
  2539.6 24.2 copy.101
  (201 shorter events, 127.1 us)
Async XLA Ops:
  7.2 566.1 %copy-start = (bf16[2048,688]{0,1:T(8,128)(2,1)S(1)}, bf16[2048,688]{0,1:T(8,128)(2,1)}, u32[]{:S(2)}) copy-start(bf16[2048,688]{0,1:T(8,128)(2,1)} %param.25) | copy-start | bytes 8454148
  7.2 180.4 %all-reduce.9.cloned.1.call-start = ((), (), s32[]{:S(2)}) async-start(), calls=%async_computation.2 | async-start | bytes 8388608 | tf_op jit(solution)/shard_map/psum | solution.py:58
  8.1 17.2 copy-start.38
  29.5 206.7 %all-gather.5.cloned.1.call-start = ((), (), s32[]{:S(2)}) async-start(), calls=%async_computation.4 | async-start | bytes 2621440 | tf_op jit(solution)/shard_map/all_gather | solution.py:71
  30.1 162.0 %copy-start.31 = (f32[2048]{0:T(1024)}, f32[2048]{0:T(1024)S(1)}, u32[]{:S(2)}) copy-start(f32[2048]{0:T(1024)S(1)} %convert_element_type.126) | copy-start | bytes 24580
  33.2 176.3 %copy-start.8 = (f32[1024,64]{1,0:T(8,128)}, f32[1024,64]{1,0:T(8,128)S(1)}, u32[]{:S(2)}) copy-start(f32[1024,64]{1,0:T(8,128)S(1)} %get-tuple-element.51) | copy-start | bytes 786436
  214.6 53.3 %all-gather.3.cloned.1.call-start = ((), (), s32[]{:S(2)}) async-start(), calls=%async_computation.3 | async-start | bytes 2621440 | tf_op jit(solution)/shard_map/all_gather | solution.py:72
  214.6 11.0 copy-start.15
  225.7 10.5 copy-start.17
  229.1 331.4 %all-reduce.11.cloned.1.call-start = ((), (), s32[]{:S(2)}) async-start(), calls=%async_computation.5 | async-start | bytes 16777216 | tf_op jit(solution)/shard_map/psum | solution.py:83
  291.8 742.8 %all-reduce.13.cloned.1.call-start = ((), (), s32[]{:S(2)}) async-start(), calls=%async_computation.6 | async-start | bytes 16777216 | tf_op jit(solution)/shard_map/psum | solution.py:90
  573.3 6.3 copy-start.44
  585.4 574.5 %reduce-scatter.3.cloned.1.call-start = ((), (), s32[]{:S(2)}) async-start(), calls=%async_computation.7 | async-start | bytes 5242880 | tf_op jit(solution)/shard_map/reduce_scatter | solution.py:113
  997.9 49.1 %copy-start.13 = (bf16[256,2048]{1,0:T(8,128)(2,1)S(1)}, bf16[256,2048]{1,0:T(8,128)(2,1)}, u32[]{:S(2)}) copy-start(bf16[256,2048]{1,0:T(8,128)(2,1)} %param.23) | copy-start | bytes 3145732
  1072.3 26.5 %copy-start.18 = (bf16[1024,2,64]{2,0,1:T(8,128)(2,1)S(1)}, bf16[1024,2,64]{2,0,1:T(8,128)(2,1)}, u32[]{:S(2)}) copy-start(bf16[1024,2,64]{2,0,1:T(8,128)(2,1)} %get-tuple-element.33) | copy-start | bytes 786436
  1072.4 26.5 %copy-start.19 = (bf16[1024,2,64]{2,0,1:T(8,128)(2,1)S(1)}, bf16[1024,2,64]{2,0,1:T(8,128)(2,1)}, u32[]{:S(2)}) copy-start(bf16[1024,2,64]{2,0,1:T(8,128)(2,1)} %get-tuple-element.34) | copy-start | bytes 786436
  1109.5 92.3 %reduce-scatter.5.cloned.1.call-start = ((), (), s32[]{:S(2)}) async-start(), calls=%async_computation.8 | async-start | bytes 5242880 | tf_op jit(solution)/shard_map/reduce_scatter | solution.py:114
  1127.9 8.5 copy-start.50
  1127.9 1411.7 %all-reduce.15.cloned.1.call-start = ((), (), s32[]{:S(2)}) async-start(), calls=%async_computation.9 | async-start | bytes 116654080 | tf_op jit(solution)/shard_map/psum | solution.py:129
  1129.2 7.2 copy-start.10
  1136.4 9.8 slice-start
  1148.8 12.3 copy-start.9
  1148.8 12.4 copy-start.20
  1175.4 32.9 %copy-start.30 = (bf16[2048,256]{1,0:T(8,128)(2,1)S(1)}, bf16[2048,256]{1,0:T(8,128)(2,1)}, u32[]{:S(2)}) copy-start(bf16[2048,256]{1,0:T(8,128)(2,1)} %param.22) | copy-start | bytes 3145732
  1201.7 6.6 copy-start.6
  1216.4 324.3 %copy-start.32 = (f32[2048]{0:T(1024)S(1)}, f32[2048]{0:T(1024)}, u32[]{:S(2)}) copy-start(f32[2048]{0:T(1024)} %copy-done.31) | copy-start | bytes 24580
  1216.4 324.3 %copy-start.34 = (f32[1024]{0:T(1024)S(1)}, f32[1024]{0:T(1024)}, u32[]{:S(2)}) copy-start(f32[1024]{0:T(1024)} %copy-done.33) | copy-start | bytes 12292
  2539.6 24.2 copy-start.24
  2539.6 25.6 copy-start.23
  2563.9 6.5 slice-start.6
  2565.2 9.6 slice-start.4
  2574.8 6.4 copy-start.1
  (39 other events, 141.0 us)
Sparse Core Ops, SparseCore 0:
  29.6 158.0 all-reduce.8
  214.7 21.4 all-gather.4
  238.3 22.3 all-gather.2
  292.0 268.4 all-reduce.10
  585.5 449.0 all-reduce.12
  1109.6 45.7 reduce-scatter.2
  1157.9 43.8 reduce-scatter.4
  1582.4 957.1 all-reduce.14
where the time goes:
time: 2600 us; the launch traced here: 2590 us
  waiting for transfers between devices  1420 us (55%)
  blocking collectives  738 us (28%)
  matrix products  195 us (8%)
  other arithmetic  135 us (5%)
  local copies, waits for them, and re-layouts  81.5 us (3%)
    psum x1, waiting for transfers between devices, device_step(): grad_table = lax.psum(table_part, 'cp')  943 us
    psum x1, blocking collectives, device_step(): d_act_b = to_bf16(lax.psum(d_act_b, 'tp'))  394 us
    psum x1, blocking collectives, device_step(): d_act_a = to_bf16(lax.psum(d_act_a, 'tp'))  324 us
    psum x1, waiting for transfers between devices, device_step(): lax.psum(jnp.dot(attended, w_o, preferred_element_type=jnp.float32), 'tp')  261 us
    psum x1, waiting for transfers between devices, device_step(): embed = lax.psum(picked, 'tp').astype(jnp.float32)  154 us
    unnamed x138, local copies, waits for them, and re-layouts  62.3 us
  transfers between devices with their start and end apart: 8, of which 6 were waited for; matrix products, arithmetic and copies ran while one was open for 5% of the time, Pallas kernels for 0%

commit v1 on v0

v1 whole, which is shorter than its diff:
```python
import functools

import jax
import jax.numpy as jnp
from jax import lax
from jax.experimental import pallas as pl
from jax.experimental.pallas import tpu as pltpu
from jax.sharding import PartitionSpec as P

NORM_EPS = 1e-5
NEG_BIG = -1e30


def rms_stats(feats):
    inv_rms = lax.rsqrt(jnp.mean(feats * feats, axis=-1, keepdims=True) + NORM_EPS)
    return feats * inv_rms, inv_rms


def rms_back(d_normed, normed, inv_rms):
    return inv_rms * (d_normed - normed * jnp.mean(d_normed * normed, axis=-1, keepdims=True))


def rotate(tensor_in, cosine, sine):
    half = tensor_in.shape[-1] // 2
    first = tensor_in[..., :half]
    second = tensor_in[..., half:]
    return jnp.concatenate([first * cosine - second * sine, second * cosine + first * sine], axis=-1)


def to_bf16(feats):
    return feats.astype(jnp.bfloat16).astype(jnp.float32)


def slot_sequence(slot, block_len, cp_count):
    shard = slot // (2 * block_len)
    within = slot % (2 * block_len)
    block_no = jnp.where(within < block_len, shard, 2 * cp_count - 1 - shard)
    return block_no * block_len + within % block_len


KEY_STEP = 512
QUERY_STEP = 256
NT = (((1,), (1,)), ((), ()))
NN = (((1,), (0,)), ((), ()))


def block_number(index, cp_count):
    shard = index // 2
    return jnp.where(index % 2 == 0, shard, 2 * cp_count - 1 - shard)


def block_scores(key_ref, query, low, high, index, cp_count, scale):
    first = block_number(index, cp_count) * KEY_STEP
    keys = key_ref[pl.ds(pl.multiple_of(index * KEY_STEP, KEY_STEP), KEY_STEP), :]
    scores = lax.dot_general(keys, query, NT, preferred_element_type=jnp.float32) * scale
    seq = first + lax.broadcasted_iota(jnp.int32, scores.shape, 0)
    return jnp.where((seq >= low) & (seq <= high), scores, NEG_BIG)


def block_needed(index, tile_low, tile_high, cp_count):
    first = block_number(index, cp_count) * KEY_STEP
    return (first <= tile_high) & (first + KEY_STEP > tile_low)


def attend_kernel(cp_count, scale, bounds, query_ref, key_ref, value_t_ref, low_ref, high_ref, out_ref, top_ref, norm_ref, scores_ref):
    tile = pl.program_id(1)
    tile_low = bounds[0, tile]
    tile_high = bounds[1, tile]
    query = query_ref[...]
    low = low_ref[...]
    high = high_ref[...]
    count = key_ref.shape[0] // KEY_STEP
    step = query.shape[0]
    top_ref[0] = jnp.full((1, step), NEG_BIG, jnp.float32)

    def rows_of(index):
        return pl.ds(pl.multiple_of(index * KEY_STEP, KEY_STEP), KEY_STEP)

    @pl.loop(0, count)
    def _(index):
        @pl.when(block_needed(index, tile_low, tile_high, cp_count))
        def _():
            scores = block_scores(key_ref, query, low, high, index, cp_count, scale)
            scores_ref[rows_of(index), :] = scores
            top_ref[0] = jnp.maximum(top_ref[0], jnp.max(scores, axis=0, keepdims=True))

    norm_ref[0] = jnp.zeros((1, step), jnp.float32)

    @pl.loop(0, count)
    def _(index):
        @pl.when(block_needed(index, tile_low, tile_high, cp_count))
        def _():
            weight = jnp.exp(scores_ref[rows_of(index), :] - top_ref[0])
            scores_ref[rows_of(index), :] = weight
            norm_ref[0] = norm_ref[0] + jnp.sum(weight, axis=0, keepdims=True)

    norm_ref[0] = 1.0 / norm_ref[0]
    out_ref[...] = jnp.zeros_like(out_ref)

    @pl.loop(0, count)
    def _(index):
        @pl.when(block_needed(index, tile_low, tile_high, cp_count))
        def _():
            prob = (scores_ref[rows_of(index), :] * norm_ref[0]).astype(jnp.bfloat16)
            out_ref[...] += lax.dot_general(value_t_ref[:, rows_of(index)], prob, NN, preferred_element_type=jnp.float32)


def attend_back_kernel(cp_count, scale, bounds, query_ref, key_ref, key_t_ref, value_ref, d_out_ref, low_ref, high_ref, top_ref, norm_ref, d_query_ref, d_kv_ref, prob_ref, d_prob_ref, dot_ref):
    tile = pl.program_id(1)
    tile_low = bounds[0, tile]
    tile_high = bounds[1, tile]
    query = query_ref[...]
    d_out = d_out_ref[...]
    low = low_ref[...]
    high = high_ref[...]
    count = key_ref.shape[0] // KEY_STEP
    step = query.shape[0]

    def rows_of(index):
        return pl.ds(pl.multiple_of(index * KEY_STEP, KEY_STEP), KEY_STEP)

    @pl.when(tile == 0)
    def _():
        d_kv_ref[...] = jnp.zeros_like(d_kv_ref)

    dot_ref[...] = jnp.zeros((1, step), jnp.float32)

    @pl.loop(0, count)
    def _(index):
        @pl.when(block_needed(index, tile_low, tile_high, cp_count))
        def _():
            scores = block_scores(key_ref, query, low, high, index, cp_count, scale)
            prob = jnp.exp(scores - top_ref[0]) * norm_ref[0]
            d_prob = lax.dot_general(value_ref[rows_of(index), :], d_out, NT, preferred_element_type=jnp.float32)
            d_prob = d_prob.astype(jnp.bfloat16).astype(jnp.float32)
            prob_ref[rows_of(index), :] = prob
            d_prob_ref[rows_of(index), :] = d_prob
            dot_ref[...] += jnp.sum(prob * d_prob, axis=0, keepdims=True)

    d_query_ref[...] = jnp.zeros_like(d_query_ref)

    @pl.loop(0, count)
    def _(index):
        @pl.when(block_needed(index, tile_low, tile_high, cp_count))
        def _():
            prob = prob_ref[rows_of(index), :]
            d_scores = prob * (d_prob_ref[rows_of(index), :] - dot_ref[...]) * scale
            d_scores = d_scores.astype(jnp.bfloat16)
            d_query_ref[...] += lax.dot_general(key_t_ref[:, rows_of(index)], d_scores, NN, preferred_element_type=jnp.float32)
            d_kv_ref[0, rows_of(index), :] += lax.dot_general(d_scores, query, NN, preferred_element_type=jnp.float32)
            d_kv_ref[1, rows_of(index), :] += lax.dot_general(prob.astype(jnp.bfloat16), d_out, NN, preferred_element_type=jnp.float32)


def attend(cp_count, scale, bounds, query, key_value, value_t, low, high):
    span, local_dim = query.shape
    total = key_value.shape[0]
    head_dim = 128
    heads = local_dim // head_dim
    step = QUERY_STEP
    tiles = span // step
    row = pl.BlockSpec((1, step), lambda h, i, b: (0, i))
    stat = pl.BlockSpec((1, 1, step), lambda h, i, b: (h, 0, i))
    out_t, top, norm = pl.pallas_call(
        functools.partial(attend_kernel, cp_count, scale),
        grid_spec=pltpu.PrefetchScalarGridSpec(
            num_scalar_prefetch=1,
            grid=(heads, tiles),
            in_specs=[
                pl.BlockSpec((step, head_dim), lambda h, i, b: (i, h)),
                pl.BlockSpec((total, head_dim), lambda h, i, b: (0, h)),
                pl.BlockSpec((head_dim, total), lambda h, i, b: (heads + h, 0)),
                row,
                row,
            ],
            out_specs=[pl.BlockSpec((head_dim, step), lambda h, i, b: (h, i)), stat, stat],
            scratch_shapes=[pltpu.VMEM((total, step), jnp.float32)],
        ),
        out_shape=[
            jax.ShapeDtypeStruct((local_dim, span), jnp.float32),
            jax.ShapeDtypeStruct((heads, 1, span), jnp.float32),
            jax.ShapeDtypeStruct((heads, 1, span), jnp.float32),
        ],
        compiler_params=pltpu.CompilerParams(vmem_limit_bytes=40 * 2**20),
        cost_estimate=pl.CostEstimate(flops=6 * span * total * local_dim, bytes_accessed=8 * total * local_dim, transcendentals=span * total * heads),
        name="attend",
    )(bounds, query, key_value, value_t, low, high)
    return out_t, top, norm


def attend_back(cp_count, scale, bounds, query, key_value, key_t, d_out, low, high, top, norm):
    span, local_dim = query.shape
    total = key_value.shape[0]
    head_dim = 128
    heads = local_dim // head_dim
    step = QUERY_STEP
    tiles = span // step
    row = pl.BlockSpec((1, step), lambda h, i, b: (0, i))
    stat = pl.BlockSpec((1, 1, step), lambda h, i, b: (h, 0, i))
    tall = pl.BlockSpec((step, head_dim), lambda h, i, b: (i, h))
    return pl.pallas_call(
        functools.partial(attend_back_kernel, cp_count, scale),
        grid_spec=pltpu.PrefetchScalarGridSpec(
            num_scalar_prefetch=1,
            grid=(heads, tiles),
            in_specs=[
                tall,
                pl.BlockSpec((total, head_dim), lambda h, i, b: (0, h)),
                pl.BlockSpec((head_dim, total), lambda h, i, b: (h, 0)),
                pl.BlockSpec((total, head_dim), lambda h, i, b: (0, heads + h)),
                tall,
                row,
                row,
                stat,
                stat,
            ],
            out_specs=[pl.BlockSpec((head_dim, step), lambda h, i, b: (h, i)), pl.BlockSpec((2, total, head_dim), lambda h, i, b: (0, 0, h))],
            scratch_shapes=[pltpu.VMEM((total, step), jnp.float32), pltpu.VMEM((total, step), jnp.float32), pltpu.VMEM((1, step), jnp.float32)],
        ),
        out_shape=[
            jax.ShapeDtypeStruct((local_dim, span), jnp.float32),
            jax.ShapeDtypeStruct((2, total, local_dim), jnp.float32),
        ],
        compiler_params=pltpu.CompilerParams(vmem_limit_bytes=48 * 2**20),
        cost_estimate=pl.CostEstimate(flops=14 * span * total * local_dim, bytes_accessed=16 * total * local_dim, transcendentals=span * total * heads),
        name="attend_back",
    )(bounds, query, key_value, key_t, key_value, d_out, low, high, top, norm)


def solution(mesh):
    cp_count = mesh.shape["cp"]
    tp_count = mesh.shape["tp"]
    core_swap = [(i, i ^ 1) for i in range(cp_count)]
    chip_swap = [(i, i ^ (cp_count // 2)) for i in range(cp_count)]

    def device_step(tokens, pos, doc_id, dy, table, w_q, w_k, w_v, w_o, w_gate, w_up, w_down, gain_one, gain_two, inv_freq):
        span = tokens.shape[0]
        part = span // tp_count
        total = span * cp_count
        rows = table.shape[0]
        width = table.shape[1]
        head_dim = 2 * inv_freq.shape[0]
        heads = w_q.shape[1] // head_dim
        local_dim = heads * head_dim
        scale = head_dim ** -0.5
        tp_rank = lax.axis_index("tp")
        cp_rank = lax.axis_index("cp")
        core = cp_rank % 2
        gain_a = gain_one.astype(jnp.float32)
        gain_b = gain_two.astype(jnp.float32)

        def cp_sum(partial):
            half = partial.shape[0] // 2
            mine = lax.dynamic_slice_in_dim(partial, core * half, half, 0)
            other = lax.dynamic_slice_in_dim(partial, (1 - core) * half, half, 0)
            chip_half = mine + lax.ppermute(other, "cp", core_swap)
            total_half = chip_half + lax.ppermute(chip_half, "cp", chip_swap)
            other_half = lax.ppermute(total_half, "cp", core_swap)
            low = jnp.where(core == 0, total_half, other_half)
            high = jnp.where(core == 0, other_half, total_half)
            return jnp.concatenate([low, high], axis=0)

        ring_order = (tp_rank - jnp.arange(tp_count)) % tp_count
        half_dim = local_dim // 2
        wo_half = lax.dynamic_slice_in_dim(w_o, core * half_dim, half_dim, 0)
        wo_parts = [wo_half]
        for shift in range(1, tp_count):
            wo_parts.append(lax.ppermute(wo_half, "tp", [(i, (i + shift) % tp_count) for i in range(tp_count)]))
        wo_mine = jnp.concatenate(wo_parts, axis=0)
        wo_other = lax.ppermute(wo_mine, "cp", core_swap)
        wo_ring = jnp.concatenate([wo_mine, wo_other], axis=0)

        def to_ring(blocks):
            picked_blocks = jnp.take(blocks, ring_order, axis=0).reshape(tp_count, part, 2, half_dim)
            both = jnp.where(core == 0, picked_blocks, picked_blocks[:, :, ::-1])
            return both.transpose(1, 2, 0, 3).reshape(part, tp_count * local_dim)

        def from_ring(flat):
            both = flat.reshape(part, 2, tp_count, half_dim).transpose(2, 0, 1, 3)
            both = jnp.where(core == 0, both, both[:, :, ::-1]).reshape(tp_count, part, local_dim)
            return jnp.take(both, ring_order, axis=0)

        local_ids = tokens - tp_rank * rows
        owned = (local_ids >= 0) & (local_ids < rows)
        safe_ids = jnp.where(owned, local_ids, 0)
        picked = jnp.where(owned[:, None], jnp.take(table, safe_ids, axis=0), jnp.zeros((), jnp.bfloat16))
        embed = lax.psum_scatter(picked, "tp", scatter_dimension=0, tiled=True).astype(jnp.float32)

        normed_a, inv_a = rms_stats(embed)
        act_a = lax.all_gather((normed_a * gain_a).astype(jnp.bfloat16), "tp", axis=0, tiled=True)
        angle = pos.astype(jnp.float32)[:, None, None] * inv_freq
        cosine = jnp.cos(angle)
        sine = jnp.sin(angle)
        query = jnp.dot(act_a, w_q, preferred_element_type=jnp.float32).reshape(span, heads, head_dim)
        query = rotate(query, cosine, sine).astype(jnp.bfloat16).reshape(span, local_dim)
        key_loc = jnp.dot(act_a, w_k, preferred_element_type=jnp.float32).reshape(span, heads, head_dim)
        key_loc = rotate(key_loc, cosine, sine).astype(jnp.bfloat16)
        value_loc = jnp.dot(act_a, w_v, preferred_element_type=jnp.float32).astype(jnp.bfloat16)
        key_value = jnp.concatenate([key_loc.reshape(span, local_dim), value_loc], axis=1)
        kv_all = lax.all_gather(key_value, "cp", axis=0, tiled=True)
        kv_all_t = kv_all.T
        token_all = lax.all_gather(tokens, "cp", axis=0, tiled=True)
        q_seq = slot_sequence(cp_rank * span + jnp.arange(span, dtype=jnp.int32), span // 2, cp_count)
        q_first = q_seq - pos
        bounds = jnp.stack([jnp.min(q_first.reshape(-1, QUERY_STEP), axis=1), jnp.max(q_seq.reshape(-1, QUERY_STEP), axis=1)])
        low = q_first.reshape(1, span)
        high = q_seq.reshape(1, span)
        out_t, top, norm = attend(cp_count, scale, bounds, query, kv_all, kv_all_t, low, high)
        attended = out_t.T.astype(jnp.bfloat16)
        att_rows = lax.all_to_all(attended.reshape(tp_count, part, local_dim), "tp", 0, 0)
        residual = embed + jnp.dot(to_ring(att_rows), wo_ring, preferred_element_type=jnp.float32)
        normed_b, inv_b = rms_stats(residual)
        act_b = lax.all_gather((normed_b * gain_b).astype(jnp.bfloat16), "tp", axis=0, tiled=True)
        gate = jnp.dot(act_b, w_gate, preferred_element_type=jnp.float32)
        up_val = jnp.dot(act_b, w_up, preferred_element_type=jnp.float32)
        gate_sig = jax.nn.sigmoid(gate)
        hidden = (gate * gate_sig * up_val).astype(jnp.bfloat16)

        d_hidden = to_bf16(jnp.einsum("td,fd->tf", dy, w_down, preferred_element_type=jnp.float32))
        d_gate = (d_hidden * up_val * gate_sig * (1.0 + gate * (1.0 - gate_sig))).astype(jnp.bfloat16)
        d_up = (d_hidden * gate * gate_sig).astype(jnp.bfloat16)
        d_act_b = jnp.einsum("tf,df->td", d_gate, w_gate, preferred_element_type=jnp.float32)
        d_act_b = d_act_b + jnp.einsum("tf,df->td", d_up, w_up, preferred_element_type=jnp.float32)
        d_act_b = to_bf16(lax.psum_scatter(d_act_b, "tp", scatter_dimension=0, tiled=True))
        grad_gain_b = jnp.sum(d_act_b * normed_b, axis=0)
        dy_part = lax.dynamic_slice_in_dim(dy, tp_rank * part, part, 0).astype(jnp.float32)
        d_resid = dy_part + rms_back(d_act_b * gain_b, normed_b, inv_b)
        d_resid_b = d_resid.astype(jnp.bfloat16)
        d_att_rows = jnp.einsum("td,cd->tc", d_resid_b, wo_ring, preferred_element_type=jnp.float32)
        d_att = lax.all_to_all(from_ring(d_att_rows.astype(jnp.bfloat16)), "tp", 0, 0)
        d_att = d_att.reshape(span, local_dim)

        hidden_late, d_att = lax.optimization_barrier((hidden, d_att))
        grad_down = cp_sum(jnp.einsum("tf,td->fd", hidden, dy, preferred_element_type=jnp.float32))
        grad_gate = cp_sum(jnp.einsum("td,tf->df", act_b, d_gate, preferred_element_type=jnp.float32))
        grad_up = cp_sum(jnp.einsum("td,tf->df", act_b, d_up, preferred_element_type=jnp.float32))
        layer_part = jnp.dot(hidden_late, w_down, preferred_element_type=jnp.float32)
        layer_part = residual + lax.psum_scatter(layer_part, "tp", scatter_dimension=0, tiled=True)
        layer_out = lax.all_gather(layer_part.astype(jnp.bfloat16), "tp", axis=0, tiled=True)
        resid_all = lax.all_gather(d_resid_b, "tp", axis=0, tiled=True)
        grad_out = cp_sum(jnp.einsum("tc,td->cd", attended, resid_all, preferred_element_type=jnp.float32))

        d_query_t, d_kv_all = attend_back(cp_count, scale, bounds, query, kv_all, kv_all_t, d_att, low, high, top, norm)
        d_query = d_query_t.T.reshape(span, heads, head_dim)
        d_kv_all = d_kv_all.reshape(2, cp_count // 2, 2, span, local_dim)
        chip = cp_rank // 2
        mate_kv = lax.dynamic_index_in_dim(d_kv_all, 1 - core, 2, keepdims=False)
        own_kv = lax.dynamic_index_in_dim(d_kv_all, core, 2, keepdims=False)
        chip_kv = own_kv + lax.ppermute(mate_kv, "cp", core_swap)
        far_kv = lax.dynamic_index_in_dim(chip_kv, 1 - chip, 1, keepdims=False)
        d_kv = lax.dynamic_index_in_dim(chip_kv, chip, 1, keepdims=False) + lax.ppermute(far_kv, "cp", chip_swap)
        d_key = d_kv[0].reshape(span, heads, head_dim)
        d_value = d_kv[1]
        d_q_pre = rotate(to_bf16(d_query), cosine, -sine)
        d_q_pre = d_q_pre.astype(jnp.bfloat16).reshape(span, local_dim)
        d_k_pre = rotate(to_bf16(d_key), cosine, -sine).astype(jnp.bfloat16).reshape(span, local_dim)
        d_v_pre = d_value.astype(jnp.bfloat16).reshape(span, local_dim)
        grad_q = cp_sum(jnp.einsum("td,tc->dc", act_a, d_q_pre, preferred_element_type=jnp.float32))
        grad_k = cp_sum(jnp.einsum("td,tc->dc", act_a, d_k_pre, preferred_element_type=jnp.float32))
        grad_v = cp_sum(jnp.einsum("td,tc->dc", act_a, d_v_pre, preferred_element_type=jnp.float32))
        d_act_a = jnp.einsum("tc,dc->td", d_q_pre, w_q, preferred_element_type=jnp.float32)
        d_act_a = d_act_a + jnp.einsum("tc,dc->td", d_k_pre, w_k, preferred_element_type=jnp.float32)
        d_act_a = d_act_a + jnp.einsum("tc,dc->td", d_v_pre, w_v, preferred_element_type=jnp.float32)
        d_act_a = to_bf16(lax.psum_scatter(d_act_a, "tp", scatter_dimension=0, tiled=True))
        grad_gain_a = jnp.sum(d_act_a * normed_a, axis=0)
        d_embed = d_resid + rms_back(d_act_a * gain_a, normed_a, inv_a)
        embed_all = lax.all_gather(d_embed, ("cp", "tp"), axis=0, tiled=True)
        all_ids = token_all - tp_rank * rows
        drop_ids = jnp.where((all_ids >= 0) & (all_ids < rows), all_ids, rows)
        grad_table = jnp.zeros((rows, width), jnp.float32).at[drop_ids].add(embed_all, mode="drop")
        gains = lax.psum(jnp.stack([grad_gain_a, grad_gain_b]), ("tp", "cp"))
        return (layer_out, grad_table, grad_q, grad_k, grad_v, grad_out, grad_gate, grad_up, grad_down, gains[0], gains[1])

    col_spec = P(None, "tp")
    row_spec = P("tp", None)
    tok_spec = P("cp")
    rep_spec = P(None)
    in_specs = (tok_spec, tok_spec, tok_spec, P("cp", None), row_spec, col_spec, col_spec, col_spec, row_spec, col_spec, col_spec, row_spec, rep_spec, rep_spec, rep_spec)
    out_specs = (P("cp", None), row_spec, col_spec, col_spec, col_spec, row_spec, col_spec, col_spec, row_spec, rep_spec, rep_spec)
    return jax.shard_map(device_step, mesh=mesh, in_specs=in_specs, out_specs=out_specs, check_vma=False)
```

time: 2600 us -> 1640 us (0.63)
  blocking collectives: 738 us -> 135 us
  waiting for transfers between devices: 1420 us -> 1010 us
  matrix products: 195 us -> 87.3 us
  starting transfers between devices: 0.97 us -> 77.1 us
  other arithmetic: 135 us -> 174 us
  Pallas kernels: 0 us -> 30.3 us
    psum x4 -> x0, waiting for transfers between devices: 1390 us -> none  [the longest x1 943 us: device_step(): grad_table = lax.psum(table_part, 'cp')]
    psum x3 -> x1, blocking collectives: 732 us -> 39.5 us  [device_step(): gains = lax.psum(jnp.stack([grad_gain_a, grad_gain_b]), ('tp', 'cp'))]
    reduce_scatter x2 -> x4, waiting for transfers between devices: 21.8 us -> 520 us  [the longest x1 148 us: device_step(): lax.psum_scatter(layer_part, 'tp', scatter_dimension=0, tiled=True)]
    ppermute x0 -> x31, waiting for transfers between devices: none -> 323 us  [the longest x7 227 us: cp_sum(): total_half = chip_half + lax.ppermute(chip_half, 'cp', chip_swap)]
    all_gather x2 -> x6, waiting for transfers between devices: 7.05 us -> 147 us  [the longest x1 77.6 us: device_step(): lax.all_gather((normed_b * gain_b).astype(jnp.bfloat16), 'tp', axis=0, ti...]
    all_gather x1, blocking collectives: 5.52 us -> 95.8 us  [device_step(): token_all = lax.all_gather(tokens, 'cp', axis=0, tiled=True)]
    dot_general x10 -> x4, matrix products: 112 us -> 22.3 us  [the longest x1 7.65 us: device_step(): jnp.dot(hidden_late, w_down, preferred_element_type=jnp.float32)]
    ppermute x0 -> x31, starting transfers between devices: none -> 40.1 us  [the longest x7 16.2 us: device_step(): lax.ppermute(wo_half, 'tp', [(i, (i + shift) % tp_count) for i in range(t...]
  transfers between devices with their start and end apart: 8 -> 43, of which waited for: 6 -> 19; matrix products, arithmetic and copies ran while one was open for 5% -> 9% of each run, Pallas kernels for 0% -> 1%
where the time goes in v1:
time: 1640 us; the launch traced here: 1630 us
  waiting for transfers between devices  1010 us (62%)
  other arithmetic  174 us (11%)
  blocking collectives  135 us (8%)
  local copies, waits for them, and re-layouts  104 us (6%)
  matrix products  87.3 us (5%)
  starting transfers between devices  77.1 us (5%)
  Pallas kernels  30.3 us (2%)
    ppermute x7, waiting for transfers between devices, cp_sum(): total_half = chip_half + lax.ppermute(chip_half, 'cp', chip_swap)  227 us
    reduce_scatter x1, waiting for transfers between devices, device_step(): lax.psum_scatter(layer_part, 'tp', scatter_dimension=0, tiled=True)  148 us
    reduce_scatter x1, waiting for transfers between devices, device_step(): lax.psum_scatter(d_act_b, 'tp', scatter_dimension=0, tiled=True)  145 us
    reduce_scatter x1, waiting for transfers between devices, device_step(): lax.psum_scatter(d_act_a, 'tp', scatter_dimension=0, tiled=True)  137 us
    all_gather x1, blocking collectives, device_step(): token_all = lax.all_gather(tokens, 'cp', axis=0, tiled=True)  95.8 us
    reduce_scatter x1, waiting for transfers between devices, device_step(): lax.psum_scatter(picked, 'tp', scatter_dimension=0, tiled=True)  90.7 us
    all_gather x1, waiting for transfers between devices, device_step(): lax.all_gather((normed_b * gain_b).astype(jnp.bfloat16), 'tp', axis=0, ti...  77.6 us
    all_gather x1, waiting for transfers between devices, device_step(): lax.all_gather((normed_a * gain_a).astype(jnp.bfloat16), 'tp', axis=0, ti...  68.9 us
  transfers between devices with their start and end apart: 43, of which 19 were waited for; matrix products, arithmetic and copies ran while one was open for 9% of the time, Pallas kernels for 1%

profile of v1, /device:TPU:0, one launch (start us, length us, event | category | flops | bytes accessed | tf_op | source)
XLA Modules:
  0.0 1633.8 jit_solution(10419347649337870287)
XLA Ops:
  8.8 16.6 %gather_fusion = bf16[1024,2048]{1,0:T(8,128)(2,1)} fusion(bf16[4032,2048]{1,0:T(8,128)(2,1)} %param.20, s32[1024]{0:T(1024)S(1)} %fusion.58), kind=kCustom, calls=%fused_computation.2 | custom fusion | bytes 8392704 | tf_op jit(solution)/shard_map/jit(_take)/gather | solution.py:285
  30.2 90.7 %reduce-scatter.5.cloned.1.call-done = bf16[128,2048]{1,0:T(8,128)(2,1)} async-done(((bf16[1024,2048]{1,0:T(8,128)(2,1)}), bf16[128,2048]{1,0:T(8,128)(2,1)}) %reduce-scatter.5.cloned.1.call-update) | async-done | bytes 524304 | tf_op jit(solution)/shard_map/reduce_scatter | solution.py:286
  127.8 68.9 %all-gather.7.cloned.1.call-done = bf16[1024,2048]{1,0:T(8,128)(2,1)} async-done(((bf16[128,2048]{1,0:T(8,128)(2,1)}), bf16[1024,2048]{1,0:T(8,128)(2,1)}) %all-gather.7.cloned.1.call-update) | async-done | bytes 4194320 | tf_op jit(solution)/shard_map/all_gather | solution.py:289
  234.3 10.8 collective-permute-done
  246.3 9.8 collective-permute-start.6
  257.1 29.7 %collective-permute-done.2 = bf16[128,2048]{1,0:T(8,128)(2,1)S(1)} collective-permute-done((bf16[128,2048]{1,0:T(8,128)(2,1)S(1)}, bf16[128,2048]{1,0:T(8,128)(2,1)S(1)}, u32[]{:S(2)}, u32[]{:S(2)}) %collective-permute-start.2) | collective-permute-done | bytes 524320 | tf_op jit(solution)/shard_map/ppermute | solution.py:267
  297.0 6.3 copy.85.value_t_ref.key_t_ref
  307.7 11.7 attend.1
  323.3 31.8 %all-to-all-start = ((bf16[8,128,256]{2,1,0:T(8,128)(2,1)}), bf16[8,128,256]{2,1,0:T(8,128)(2,1)}, u32[]{:S(2)}, u32[]{:S(2)}) async-start(bf16[8,128,256]{2,1,0:T(8,128)(2,1)} %bitcast.106), calls=%async_computation.1 | async-start | bytes 1048576 | tf_op jit(solution)/shard_map/all_to_all | solution.py:309
  382.4 7.3 convolution_convert_fusion.1
  389.6 77.6 %all-gather.11.cloned.1.call-done = bf16[1024,2048]{1,0:T(8,128)(2,1)} async-done(((bf16[128,2048]{1,0:T(8,128)(2,1)}), bf16[1024,2048]{1,0:T(8,128)(2,1)}) %all-gather.11.cloned.1.call-update) | async-done | bytes 4194320 | tf_op jit(solution)/shard_map/all_gather | solution.py:312
  488.2 144.7 %reduce-scatter.7.cloned.1.call-done = f32[128,2048]{1,0:T(8,128)} async-done(((f32[1024,2048]{1,0:T(8,128)}), f32[128,2048]{1,0:T(8,128)}) %reduce-scatter.7.cloned.1.call-update) | async-done | bytes 1048592 | tf_op jit(solution)/shard_map/reduce_scatter | solution.py:323
  636.2 6.4 convolution_convert_fusion
  648.9 14.5 all-to-all-done.1
  663.5 18.6 %attend_back.1 = (f32[256,1024]{1,0:T(8,128)S(1)}, f32[2,4096,256]{2,1,0:T(8,128)}) custom-call(s32[2,4]{1,0:T(2,128)S(1)} %pad_add_fusion.bounds, bf16[1024,256]{1,0:T(8,128)(2,1)S(1)} %bitcast.94, bf16[4096,512]{1,0:T(8,128)(2,1)} %all-gather.9.cloned.1.call-done.key_ref.value_ref, bf16[512,4096]{1,0:T(8,128)(2,1)} %copy.85.value_t_ref.key_t_ref, ...), custom_call_target="tpu_custom_call" | custom-call | flops 15032385536 | bytes 16777216 | tf_op jit(solution)/shard_map/attend_back/pallas_call | solution.py:200
  686.7 13.5 collective-permute-start.8
  700.2 6.8 collective-permute-done.8
  717.3 45.0 %collective-permute-done.9 = f32[2,1024,256]{2,1,0:T(8,128)} collective-permute-done((f32[2,1024,256]{2,1,0:T(8,128)}, f32[2,1024,256]{2,1,0:T(8,128)}, u32[]{:S(2)}, u32[]{:S(2)}) %collective-permute-start.9) | collective-permute-done | bytes 2097184 | tf_op jit(solution)/shard_map/ppermute | solution.py:350
  784.7 7.6 fusion.73
  793.2 136.6 %reduce-scatter.11.cloned.1.call-done = f32[128,2048]{1,0:T(8,128)} async-done(((f32[1024,2048]{1,0:T(8,128)}), f32[128,2048]{1,0:T(8,128)}) %reduce-scatter.11.cloned.1.call-update) | async-done | bytes 1048592 | tf_op jit(solution)/shard_map/reduce_scatter | solution.py:363
  931.4 148.0 %reduce-scatter.9.cloned.1.call-done = f32[128,2048]{1,0:T(8,128)} async-done(((f32[1024,2048]{1,0:T(8,128)}), f32[128,2048]{1,0:T(8,128)}) %reduce-scatter.9.cloned.1.call-update) | async-done | bytes 1048592 | tf_op jit(solution)/shard_map/reduce_scatter | solution.py:337
  1101.5 6.2 fusion.61
  1124.9 52.9 %collective-permute-done.29 = f32[344,2048]{1,0:T(8,128)} collective-permute-done((f32[344,2048]{1,0:T(8,128)S(1)}, f32[344,2048]{1,0:T(8,128)}, u32[]{:S(2)}, u32[]{:S(2)}) %collective-permute-start.29) | collective-permute-done | bytes 2818080 | tf_op jit(solution)/shard_map/ppermute | solution.py:256
  1180.0 58.1 %collective-permute-done.23 = f32[1024,688]{0,1:T(8,128)S(1)} collective-permute-done((f32[1024,688]{0,1:T(8,128)S(1)}, f32[1024,688]{0,1:T(8,128)S(1)}, u32[]{:S(2)}, u32[]{:S(2)}) %collective-permute-start.23) | collective-permute-done | bytes 2818080 | tf_op jit(solution)/shard_map/ppermute | solution.py:256
  1240.2 95.8 %all_gather.25 = s32[4096]{0:T(1024)S(1)} all-gather(s32[1024]{0:T(1024)S(1)} %copy-done.40), channel_id=1, replica_groups=mesh['tp'=8,'cp'=4] {'cp'}, dimensions={0}, use_global_device_ids=true | all-gather | bytes 20480 | tf_op jit(solution)/shard_map/all_gather | solution.py:301
  1346.7 6.5 broadcast_select_fusion.5
  1380.9 41.0 %collective-permute-done.11 = f32[1024,256]{1,0:T(8,128)S(1)} collective-permute-done((f32[1024,256]{1,0:T(8,128)S(1)}, f32[1024,256]{1,0:T(8,128)S(1)}, u32[]{:S(2)}, u32[]{:S(2)}) %collective-permute-start.11) | collective-permute-done | bytes 1048608 | tf_op jit(solution)/shard_map/ppermute | solution.py:256
  1425.2 38.7 %collective-permute-done.14 = f32[1024,256]{1,0:T(8,128)S(1)} collective-permute-done((f32[1024,256]{1,0:T(8,128)S(1)}, f32[1024,256]{1,0:T(8,128)S(1)}, u32[]{:S(2)}, u32[]{:S(2)}) %collective-permute-start.14) | collective-permute-done | bytes 1048608 | tf_op jit(solution)/shard_map/ppermute | solution.py:256
  1471.9 14.5 collective-permute-done.17
  1486.6 22.0 %collective-permute-done.20 = f32[128,2048]{1,0:T(8,128)S(1)} collective-permute-done((f32[128,2048]{1,0:T(8,128)S(1)}, f32[128,2048]{1,0:T(8,128)S(1)}, u32[]{:S(2)}, u32[]{:S(2)}) %collective-permute-start.20) | collective-permute-done | bytes 1048608 | tf_op jit(solution)/shard_map/ppermute | solution.py:256
  1515.5 39.5 %psum.7 = f32[2,2048]{1,0:T(2,128)S(1)} all-reduce(f32[2,2048]{1,0:T(2,128)S(1)} %pad_maximum_fusion.12), channel_id=1, replica_groups=mesh['tp'=8,'cp'=4] {'tp','cp'}, use_global_device_ids=true, to_apply=%region_13.15 | all-reduce | flops 4096 | bytes 32768 | tf_op jit(solution)/shard_map/psum | solution.py:370
  1555.6 65.9 %scatter_custom_fusion = f32[4032,2048]{1,0:T(8,128)} fusion(s32[4096]{0:T(1024)S(1)} %compare_select_fusion, f32[4096,2048]{1,0:T(8,128)} %all-gather.15.cloned.1.call-done, f32[]{:T(128)} %constant.160.clone.1), kind=kCustom, calls=%fused_computation.4 | custom fusion | flops 8388608 | bytes 33030656 | tf_op jit(solution)/shard_map/scatter-add | solution.py:369
  (310 shorter events, 274.1 us)
Async XLA Ops:
  7.2 113.7 %reduce-scatter.5.cloned.1.call-start = ((), (), s32[]{:S(2)}) async-start(), calls=%async_computation.6 | async-start | bytes 4718592 | tf_op jit(solution)/shard_map/reduce_scatter | solution.py:286
  29.5 167.2 %all-gather.7.cloned.1.call-start = ((), (), s32[]{:S(2)}) async-start(), calls=%async_computation.7 | async-start | bytes 4718592 | tf_op jit(solution)/shard_map/all_gather | solution.py:289
  124.2 172.8 %all-gather.9.cloned.1.call-start = ((), (), s32[]{:S(2)}) async-start(), calls=%async_computation.8 | async-start | bytes 5242880 | tf_op jit(solution)/shard_map/all_gather | solution.py:299
  228.2 58.7 %collective-permute-start.2 = (bf16[128,2048]{1,0:T(8,128)(2,1)S(1)}, bf16[128,2048]{1,0:T(8,128)(2,1)S(1)}, u32[]{:S(2)}, u32[]{:S(2)}) collective-permute-start(bf16[128,2048]{1,0:T(8,128)(2,1)S(1)} %get-tuple-element.31), channel_id=1, source_target_pairs={{0,12},{4,16},{8,20},{12,24},{16,28},{20,0},{24,4},{28,8},{1,13},{... | collective-permute-start | bytes 1572872 | tf_op jit(solution)/shard_map/ppermute | solution.py:267
  230.5 57.4 %collective-permute-start.3 = (bf16[128,2048]{1,0:T(8,128)(2,1)S(1)}, bf16[128,2048]{1,0:T(8,128)(2,1)S(1)}, u32[]{:S(2)}, u32[]{:S(2)}) collective-permute-start(bf16[128,2048]{1,0:T(8,128)(2,1)S(1)} %get-tuple-element.31), channel_id=1, source_target_pairs={{0,16},{4,20},{8,24},{12,28},{16,0},{20,4},{24,8},{28,12},{1,17},{... | collective-permute-start | bytes 1572872 | tf_op jit(solution)/shard_map/ppermute | solution.py:267
  232.9 56.1 %collective-permute-start.4 = (bf16[128,2048]{1,0:T(8,128)(2,1)S(1)}, bf16[128,2048]{1,0:T(8,128)(2,1)S(1)}, u32[]{:S(2)}, u32[]{:S(2)}) collective-permute-start(bf16[128,2048]{1,0:T(8,128)(2,1)S(1)} %get-tuple-element.31), channel_id=1, source_target_pairs={{0,20},{4,24},{8,28},{12,0},{16,4},{20,8},{24,12},{28,16},{1,21},{... | collective-permute-start | bytes 1572872 | tf_op jit(solution)/shard_map/ppermute | solution.py:267
  245.2 45.0 %collective-permute-start.5 = (bf16[128,2048]{1,0:T(8,128)(2,1)S(1)}, bf16[128,2048]{1,0:T(8,128)(2,1)S(1)}, u32[]{:S(2)}, u32[]{:S(2)}) collective-permute-start(bf16[128,2048]{1,0:T(8,128)(2,1)S(1)} %get-tuple-element.31), channel_id=1, source_target_pairs={{0,24},{4,28},{8,0},{12,4},{16,8},{20,12},{24,16},{28,20},{1,25},{... | collective-permute-start | bytes 1572872 | tf_op jit(solution)/shard_map/ppermute | solution.py:267
  246.3 48.1 %collective-permute-start.6 = (bf16[128,2048]{1,0:T(8,128)(2,1)S(1)}, bf16[128,2048]{1,0:T(8,128)(2,1)S(1)}, u32[]{:S(2)}, u32[]{:S(2)}) collective-permute-start(bf16[128,2048]{1,0:T(8,128)(2,1)S(1)} %get-tuple-element.31), channel_id=1, source_target_pairs={{0,28},{4,0},{8,4},{12,8},{16,12},{20,16},{24,20},{28,24},{1,29},{... | collective-permute-start | bytes 1572872 | tf_op jit(solution)/shard_map/ppermute | solution.py:267
  295.5 59.9 %collective-permute-start.7 = (bf16[1024,2048]{1,0:T(8,128)(2,1)}, bf16[1024,2048]{1,0:T(8,128)(2,1)}, u32[]{:S(2)}, u32[]{:S(2)}) collective-permute-start(bf16[1024,2048]{1,0:T(8,128)(2,1)} %get-tuple-element.68), channel_id=1, source_target_pairs={{0,1},{1,0},{2,3},{3,2},{4,5},{5,4},{6,7},{7,6},{8,9},{9,8},{10,11... | collective-permute-start | bytes 12582920 | tf_op jit(solution)/shard_map/ppermute | solution.py:269
  323.3 42.5 %all-to-all-start = ((bf16[8,128,256]{2,1,0:T(8,128)(2,1)}), bf16[8,128,256]{2,1,0:T(8,128)(2,1)}, u32[]{:S(2)}, u32[]{:S(2)}) async-start(bf16[8,128,256]{2,1,0:T(8,128)(2,1)} %bitcast.106), calls=%async_computation.1 | async-start | bytes 1048576 | tf_op jit(solution)/shard_map/all_to_all | solution.py:309
  355.1 112.2 %all-gather.11.cloned.1.call-start = ((), (), s32[]{:S(2)}) async-start(), calls=%async_computation.9 | async-start | bytes 4718592 | tf_op jit(solution)/shard_map/all_gather | solution.py:312
  382.3 250.5 %reduce-scatter.7.cloned.1.call-start = ((), (), s32[]{:S(2)}) async-start(), calls=%async_computation.10 | async-start | bytes 9437184 | tf_op jit(solution)/shard_map/reduce_scatter | solution.py:323
  648.8 281.0 %reduce-scatter.11.cloned.1.call-start = ((), (), s32[]{:S(2)}) async-start(), calls=%async_computation.13 | async-start | bytes 9437184 | tf_op jit(solution)/shard_map/reduce_scatter | solution.py:363
  686.7 20.3 %collective-permute-start.8 = (f32[2,2,1024,256]{3,2,1,0:T(8,128)}, f32[2,2,1024,256]{3,2,1,0:T(8,128)}, u32[]{:S(2)}, u32[]{:S(2)}) collective-permute-start(f32[2,2,1024,256]{3,2,1,0:T(8,128)} %dynamic-slice_bitcast_fusion), channel_id=1, source_target_pairs={{0,1},{1,0},{2,3},{3,2},{4,5},{5,4},{6,7},{7,6},{8,9},{9,8},{10,11... | collective-permute-start | bytes 12582920 | tf_op jit(solution)/shard_map/ppermute | solution.py:348
  714.5 47.9 %collective-permute-start.9 = (f32[2,1024,256]{2,1,0:T(8,128)}, f32[2,1024,256]{2,1,0:T(8,128)}, u32[]{:S(2)}, u32[]{:S(2)}) collective-permute-start(f32[2,1024,256]{2,1,0:T(8,128)} %dynamic-slice_bitcast_fusion.1), channel_id=1, source_target_pairs={{0,2},{1,3},{2,0},{3,1},{4,6},{5,7},{6,4},{7,5},{8,10},{9,11},{10,... | collective-permute-start | bytes 6291464 | tf_op jit(solution)/shard_map/ppermute | solution.py:350
  783.4 296.1 %reduce-scatter.9.cloned.1.call-start = ((), (), s32[]{:S(2)}) async-start(), calls=%async_computation.11 | async-start | bytes 9437184 | tf_op jit(solution)/shard_map/reduce_scatter | solution.py:337
  792.4 572.0 %all-gather.17.cloned.1.call-start = ((), (), s32[]{:S(2)}) async-start(), calls=%async_computation.15 | async-start | bytes 4718592 | tf_op jit(solution)/shard_map/all_gather | solution.py:339
  793.1 762.4 %all-gather.13.cloned.1.call-start = ((), (), s32[]{:S(2)}) async-start(), calls=%async_computation.12 | async-start | bytes 4718592 | tf_op jit(solution)/shard_map/all_gather | solution.py:338
  1082.8 472.7 %all-gather.15.cloned.1.call-start = ((), (), s32[]{:S(2)}) async-start(), calls=%async_computation.14 | async-start | bytes 34603008 | tf_op jit(solution)/shard_map/all_gather | solution.py:366
  1113.7 64.0 %collective-permute-start.29 = (f32[344,2048]{1,0:T(8,128)S(1)}, f32[344,2048]{1,0:T(8,128)}, u32[]{:S(2)}, u32[]{:S(2)}) collective-permute-start(f32[344,2048]{1,0:T(8,128)S(1)} %dynamic-slice_add_fusion), channel_id=1, source_target_pairs={{0,2},{1,3},{2,0},{3,1},{4,6},{5,7},{6,4},{7,5},{8,10},{9,11},{10,... | collective-permute-start | bytes 8454152 | tf_op jit(solution)/shard_map/ppermute | solution.py:256
  1118.7 119.4 %collective-permute-start.23 = (f32[1024,688]{0,1:T(8,128)S(1)}, f32[1024,688]{0,1:T(8,128)S(1)}, u32[]{:S(2)}, u32[]{:S(2)}) collective-permute-start(f32[1024,688]{0,1:T(8,128)S(1)} %dynamic-slice_add_fusion.2), channel_id=1, source_target_pairs={{0,2},{1,3},{2,0},{3,1},{4,6},{5,7},{6,4},{7,5},{8,10},{9,11},{10,... | collective-permute-start | bytes 8454152 | tf_op jit(solution)/shard_map/ppermute | solution.py:256
  1123.6 212.4 %collective-permute-start.26 = (f32[1024,688]{0,1:T(8,128)}, f32[1024,688]{0,1:T(8,128)}, u32[]{:S(2)}, u32[]{:S(2)}) collective-permute-start(f32[1024,688]{0,1:T(8,128)} %dynamic-slice_add_fusion.1), channel_id=1, source_target_pairs={{0,2},{1,3},{2,0},{3,1},{4,6},{5,7},{6,4},{7,5},{8,10},{9,11},{10,... | collective-permute-start | bytes 8454152 | tf_op jit(solution)/shard_map/ppermute | solution.py:256
  1179.9 161.5 %collective-permute-start.30 = (f32[344,2048]{1,0:T(8,128)S(1)}, f32[344,2048]{1,0:T(8,128)}, u32[]{:S(2)}, u32[]{:S(2)}) collective-permute-start(f32[344,2048]{1,0:T(8,128)S(1)} %add.325), channel_id=1, source_target_pairs={{0,1},{1,0},{2,3},{3,2},{4,5},{5,4},{6,7},{7,6},{8,9},{9,8},{10,11... | collective-permute-start | bytes 8454152 | tf_op jit(solution)/shard_map/ppermute | solution.py:257
  1240.2 106.4 %collective-permute-start.24 = (f32[1024,688]{0,1:T(8,128)}, f32[1024,688]{0,1:T(8,128)}, u32[]{:S(2)}, u32[]{:S(2)}) collective-permute-start(f32[1024,688]{0,1:T(8,128)} %add.319), channel_id=1, source_target_pairs={{0,1},{1,0},{2,3},{3,2},{4,5},{5,4},{6,7},{7,6},{8,9},{9,8},{10,11... | collective-permute-start | bytes 8454152 | tf_op jit(solution)/shard_map/ppermute | solution.py:257
  1341.1 27.3 %collective-permute-start.27 = (f32[1024,688]{0,1:T(8,128)}, f32[1024,688]{0,1:T(8,128)}, u32[]{:S(2)}, u32[]{:S(2)}) collective-permute-start(f32[1024,688]{0,1:T(8,128)} %add.321), channel_id=1, source_target_pairs={{0,1},{1,0},{2,3},{3,2},{4,5},{5,4},{6,7},{7,6},{8,9},{9,8},{10,11... | collective-permute-start | bytes 8454152 | tf_op jit(solution)/shard_map/ppermute | solution.py:257
  1373.4 48.6 %collective-permute-start.11 = (f32[1024,256]{1,0:T(8,128)S(1)}, f32[1024,256]{1,0:T(8,128)S(1)}, u32[]{:S(2)}, u32[]{:S(2)}) collective-permute-start(f32[1024,256]{1,0:T(8,128)S(1)} %dynamic-slice_add_fusion.6), channel_id=1, source_target_pairs={{0,2},{1,3},{2,0},{3,1},{4,6},{5,7},{6,4},{7,5},{8,10},{9,11},{10,... | collective-permute-start | bytes 3145736 | tf_op jit(solution)/shard_map/ppermute | solution.py:256
  1376.3 87.6 %collective-permute-start.14 = (f32[1024,256]{1,0:T(8,128)S(1)}, f32[1024,256]{1,0:T(8,128)S(1)}, u32[]{:S(2)}, u32[]{:S(2)}) collective-permute-start(f32[1024,256]{1,0:T(8,128)S(1)} %dynamic-slice_add_fusion.5), channel_id=1, source_target_pairs={{0,2},{1,3},{2,0},{3,1},{4,6},{5,7},{6,4},{7,5},{8,10},{9,11},{10,... | collective-permute-start | bytes 3145736 | tf_op jit(solution)/shard_map/ppermute | solution.py:256
  1378.6 107.7 %collective-permute-start.17 = (f32[1024,256]{1,0:T(8,128)S(1)}, f32[1024,256]{1,0:T(8,128)S(1)}, u32[]{:S(2)}, u32[]{:S(2)}) collective-permute-start(f32[1024,256]{1,0:T(8,128)S(1)} %dynamic-slice_add_fusion.4), channel_id=1, source_target_pairs={{0,2},{1,3},{2,0},{3,1},{4,6},{5,7},{6,4},{7,5},{8,10},{9,11},{10,... | collective-permute-start | bytes 3145736 | tf_op jit(solution)/shard_map/ppermute | solution.py:256
  1380.1 128.4 %collective-permute-start.20 = (f32[128,2048]{1,0:T(8,128)S(1)}, f32[128,2048]{1,0:T(8,128)S(1)}, u32[]{:S(2)}, u32[]{:S(2)}) collective-permute-start(f32[128,2048]{1,0:T(8,128)S(1)} %dynamic-slice_add_fusion.3), channel_id=1, source_target_pairs={{0,2},{1,3},{2,0},{3,1},{4,6},{5,7},{6,4},{7,5},{8,10},{9,11},{10,... | collective-permute-start | bytes 3145736 | tf_op jit(solution)/shard_map/ppermute | solution.py:256
  1422.1 86.7 %collective-permute-start.12 = (f32[1024,256]{1,0:T(8,128)S(1)}, f32[1024,256]{1,0:T(8,128)S(1)}, u32[]{:S(2)}, u32[]{:S(2)}) collective-permute-start(f32[1024,256]{1,0:T(8,128)S(1)} %add.310), channel_id=1, source_target_pairs={{0,1},{1,0},{2,3},{3,2},{4,5},{5,4},{6,7},{7,6},{8,9},{9,8},{10,11... | collective-permute-start | bytes 3145736 | tf_op jit(solution)/shard_map/ppermute | solution.py:257
  1464.0 44.9 %collective-permute-start.15 = (f32[1024,256]{1,0:T(8,128)S(1)}, f32[1024,256]{1,0:T(8,128)S(1)}, u32[]{:S(2)}, u32[]{:S(2)}) collective-permute-start(f32[1024,256]{1,0:T(8,128)S(1)} %add.312), channel_id=1, source_target_pairs={{0,1},{1,0},{2,3},{3,2},{4,5},{5,4},{6,7},{7,6},{8,9},{9,8},{10,11... | collective-permute-start | bytes 3145736 | tf_op jit(solution)/shard_map/ppermute | solution.py:257
  1486.5 25.7 %collective-permute-start.18 = (f32[1024,256]{1,0:T(8,128)S(1)}, f32[1024,256]{1,0:T(8,128)S(1)}, u32[]{:S(2)}, u32[]{:S(2)}) collective-permute-start(f32[1024,256]{1,0:T(8,128)S(1)} %add.314), channel_id=1, source_target_pairs={{0,1},{1,0},{2,3},{3,2},{4,5},{5,4},{6,7},{7,6},{8,9},{9,8},{10,11... | collective-permute-start | bytes 3145736 | tf_op jit(solution)/shard_map/ppermute | solution.py:257
  (64 other events, 1980.5 us)
Sparse Core Ops, SparseCore 0:
  29.7 91.1 reduce-scatter.4
  124.3 72.4 all-gather.6
  225.2 32.3 all-gather.8
  382.4 84.8 all-gather.10
  488.3 144.5 reduce-scatter.6
  783.5 146.2 reduce-scatter.10
  933.4 145.9 reduce-scatter.8
  1081.6 72.5 all-gather.16
  1156.3 71.1 all-gather.12
  1230.4 267.4 all-gather.14

commit v2 on v1

--- a/solution.py
+++ b/solution.py
@@ -6,6 +6,7 @@
 from jax.experimental import pallas as pl
 from jax.experimental.pallas import tpu as pltpu
 from jax.sharding import PartitionSpec as P
+
 
 NORM_EPS = 1e-5
 NEG_BIG = -1e30
@@ -235,7 +236,6 @@
     def device_step(tokens, pos, doc_id, dy, table, w_q, w_k, w_v, w_o, w_gate, w_up, w_down, gain_one, gain_two, inv_freq):
         span = tokens.shape[0]
         part = span // tp_count
-        total = span * cp_count
         rows = table.shape[0]
         width = table.shape[1]
         head_dim = 2 * inv_freq.shape[0]
@@ -252,8 +252,10 @@
             half = partial.shape[0] // 2
             mine = lax.dynamic_slice_in_dim(partial, core * half, half, 0)
             other = lax.dynamic_slice_in_dim(partial, (1 - core) * half, half, 0)
-            chip_half = mine + lax.ppermute(other, "cp", core_swap)
-            total_half = chip_half + lax.ppermute(chip_half, "cp", chip_swap)
+            mate_part = lax.ppermute(other, "cp", core_swap)
+            chip_half = mine + mate_part
+            far_part = lax.ppermute(chip_half, "cp", chip_swap)
+            total_half = chip_half + far_part
             other_half = lax.ppermute(total_half, "cp", core_swap)
             low = jnp.where(core == 0, total_half, other_half)
             high = jnp.where(core == 0, other_half, total_half)
@@ -320,7 +322,8 @@
         d_up = (d_hidden * gate * gate_sig).astype(jnp.bfloat16)
         d_act_b = jnp.einsum("tf,df->td", d_gate, w_gate, preferred_element_type=jnp.float32)
         d_act_b = d_act_b + jnp.einsum("tf,df->td", d_up, w_up, preferred_element_type=jnp.float32)
-        d_act_b = to_bf16(lax.psum_scatter(d_act_b, "tp", scatter_dimension=0, tiled=True))
+        d_act_b = lax.psum_scatter(d_act_b, "tp", scatter_dimension=0, tiled=True)
+        d_act_b = to_bf16(d_act_b)
         grad_gain_b = jnp.sum(d_act_b * normed_b, axis=0)
         dy_part = lax.dynamic_slice_in_dim(dy, tp_rank * part, part, 0).astype(jnp.float32)
         d_resid = dy_part + rms_back(d_act_b * gain_b, normed_b, inv_b)
@@ -329,13 +332,12 @@
         d_att = lax.all_to_all(from_ring(d_att_rows.astype(jnp.bfloat16)), "tp", 0, 0)
         d_att = d_att.reshape(span, local_dim)
 
-        hidden_late, d_att = lax.optimization_barrier((hidden, d_att))
+        hidden_late = hidden
         grad_down = cp_sum(jnp.einsum("tf,td->fd", hidden, dy, preferred_element_type=jnp.float32))
         grad_gate = cp_sum(jnp.einsum("td,tf->df", act_b, d_gate, preferred_element_type=jnp.float32))
         grad_up = cp_sum(jnp.einsum("td,tf->df", act_b, d_up, preferred_element_type=jnp.float32))
         layer_part = jnp.dot(hidden_late, w_down, preferred_element_type=jnp.float32)
-        layer_part = residual + lax.psum_scatter(layer_part, "tp", scatter_dimension=0, tiled=True)
-        layer_out = lax.all_gather(layer_part.astype(jnp.bfloat16), "tp", axis=0, tiled=True)
+        layer_sum = lax.psum_scatter(layer_part, "tp", scatter_dimension=0, tiled=True)
         resid_all = lax.all_gather(d_resid_b, "tp", axis=0, tiled=True)
         grad_out = cp_sum(jnp.einsum("tc,td->cd", attended, resid_all, preferred_element_type=jnp.float32))
 
@@ -360,7 +362,11 @@
         d_act_a = jnp.einsum("tc,dc->td", d_q_pre, w_q, preferred_element_type=jnp.float32)
         d_act_a = d_act_a + jnp.einsum("tc,dc->td", d_k_pre, w_k, preferred_element_type=jnp.float32)
         d_act_a = d_act_a + jnp.einsum("tc,dc->td", d_v_pre, w_v, preferred_element_type=jnp.float32)
-        d_act_a = to_bf16(lax.psum_scatter(d_act_a, "tp", scatter_dimension=0, tiled=True))
+        d_act_a, layer_sum = lax.optimization_barrier((d_act_a, layer_sum))
+        d_act_a = lax.psum_scatter(d_act_a, "tp", scatter_dimension=0, tiled=True)
+        d_act_a = to_bf16(d_act_a)
+        layer_part = residual + layer_sum
+        layer_out = lax.all_gather(layer_part.astype(jnp.bfloat16), "tp", axis=0, tiled=True)
         grad_gain_a = jnp.sum(d_act_a * normed_a, axis=0)
         d_embed = d_resid + rms_back(d_act_a * gain_a, normed_a, inv_a)
         embed_all = lax.all_gather(d_embed, ("cp", "tp"), axis=0, tiled=True)
@@ -376,4 +382,5 @@
     rep_spec = P(None)
     in_specs = (tok_spec, tok_spec, tok_spec, P("cp", None), row_spec, col_spec, col_spec, col_spec, row_spec, col_spec, col_spec, row_spec, rep_spec, rep_spec, rep_spec)
     out_specs = (P("cp", None), row_spec, col_spec, col_spec, col_spec, row_spec, col_spec, col_spec, row_spec, rep_spec, rep_spec)
+
     return jax.shard_map(device_step, mesh=mesh, in_specs=in_specs, out_specs=out_specs, check_vma=False)

time: 1640 us -> 1500 us (0.915)
  waiting for transfers between devices: 1010 us -> 878 us
    reduce_scatter x1, waiting for transfers between devices: 148 us -> 3.93 us  [device_step(): lax.psum_scatter(layer_part, 'tp', scatter_dimension=0, tiled=True)]
  transfers between devices with their start and end apart: 43 -> 43, of which waited for: 19 -> 19; matrix products, arithmetic and copies ran while one was open for 9% -> 12% of each run, Pallas kernels for 1% -> 2%
where the time goes in v2:
time: 1500 us
  waiting for transfers between devices  878 us (59%)
  other arithmetic  174 us (12%)
  blocking collectives  135 us (9%)
  local copies, waits for them, and re-layouts  105 us (7%)
  matrix products  86.7 us (6%)
  starting transfers between devices  73.3 us (5%)
  Pallas kernels  29.9 us (2%)
  between operations  15.5 us (1%)
    ppermute x7, waiting for transfers between devices, cp_sum(): far_part = lax.ppermute(chip_half, 'cp', chip_swap)  225 us
    reduce_scatter x1, waiting for transfers between devices, device_step(): d_act_a = lax.psum_scatter(d_act_a, 'tp', scatter_dimension=0, tiled=True)  150 us
    reduce_scatter x1, waiting for transfers between devices, device_step(): d_act_b = lax.psum_scatter(d_act_b, 'tp', scatter_dimension=0, tiled=True)  137 us
    all_gather x1, blocking collectives, device_step(): token_all = lax.all_gather(tokens, 'cp', axis=0, tiled=True)  95.4 us
    reduce_scatter x1, waiting for transfers between devices, device_step(): lax.psum_scatter(picked, 'tp', scatter_dimension=0, tiled=True)  90.5 us
    all_gather x1, waiting for transfers between devices, device_step(): lax.all_gather((normed_a * gain_a).astype(jnp.bfloat16), 'tp', axis=0, ti...  69.2 us
    all_gather x1, waiting for transfers between devices, device_step(): lax.all_gather((normed_b * gain_b).astype(jnp.bfloat16), 'tp', axis=0, ti...  67.3 us
    scatter-add x1, other arithmetic, device_step(): jnp.zeros((rows, width), jnp.float32).at[drop_ids]  65.8 us
  transfers between devices with their start and end apart: 43, of which 19 were waited for; matrix products, arithmetic and copies ran while one was open for 12% of the time, Pallas kernels for 2%

profile of v2, /device:TPU:0, one launch (start us, length us, event | category | flops | bytes accessed | tf_op | source)
XLA Modules:
  0.0 1496.4 jit_solution(17895949198049701865)
XLA Ops:
  8.8 16.6 %gather_fusion = bf16[1024,2048]{1,0:T(8,128)(2,1)} fusion(bf16[4032,2048]{1,0:T(8,128)(2,1)} %param.20, s32[1024]{0:T(1024)S(1)} %fusion.58), kind=kCustom, calls=%fused_computation.2 | custom fusion | bytes 8392704 | tf_op jit(solution)/shard_map/jit(_take)/gather | solution.py:287
  30.2 90.5 %reduce-scatter.5.cloned.1.call-done = bf16[128,2048]{1,0:T(8,128)(2,1)} async-done(((bf16[1024,2048]{1,0:T(8,128)(2,1)}), bf16[128,2048]{1,0:T(8,128)(2,1)}) %reduce-scatter.5.cloned.1.call-update) | async-done | bytes 524304 | tf_op jit(solution)/shard_map/reduce_scatter | solution.py:288
  127.4 69.2 %all-gather.7.cloned.1.call-done = bf16[1024,2048]{1,0:T(8,128)(2,1)} async-done(((bf16[128,2048]{1,0:T(8,128)(2,1)}), bf16[1024,2048]{1,0:T(8,128)(2,1)}) %all-gather.7.cloned.1.call-update) | async-done | bytes 4194320 | tf_op jit(solution)/shard_map/all_gather | solution.py:291
  234.5 10.0 collective-permute-done
  245.6 9.6 collective-permute-start.6
  256.3 30.8 %collective-permute-done.2 = bf16[128,2048]{1,0:T(8,128)(2,1)S(1)} collective-permute-done((bf16[128,2048]{1,0:T(8,128)(2,1)S(1)}, bf16[128,2048]{1,0:T(8,128)(2,1)S(1)}, u32[]{:S(2)}, u32[]{:S(2)}) %collective-permute-start.2) | collective-permute-done | bytes 524320 | tf_op jit(solution)/shard_map/ppermute | solution.py:269
  296.6 6.3 copy.85.value_t_ref.key_t_ref
  307.3 11.7 attend.1
  322.9 32.4 %all-to-all-start = ((bf16[8,128,256]{2,1,0:T(8,128)(2,1)}), bf16[8,128,256]{2,1,0:T(8,128)(2,1)}, u32[]{:S(2)}, u32[]{:S(2)}) async-start(bf16[8,128,256]{2,1,0:T(8,128)(2,1)} %bitcast.106), calls=%async_computation.1 | async-start | bytes 1048576 | tf_op jit(solution)/shard_map/all_to_all | solution.py:311
  360.2 9.7 all-to-all-done
  386.8 7.3 convolution_convert_fusion.1
  394.1 67.3 %all-gather.11.cloned.1.call-done = bf16[1024,2048]{1,0:T(8,128)(2,1)} async-done(((bf16[128,2048]{1,0:T(8,128)(2,1)}), bf16[1024,2048]{1,0:T(8,128)(2,1)}) %all-gather.11.cloned.1.call-update) | async-done | bytes 4194320 | tf_op jit(solution)/shard_map/all_gather | solution.py:314
  484.0 7.1 fusion.73
  491.1 137.3 %reduce-scatter.7.cloned.1.call-done = f32[128,2048]{1,0:T(8,128)} async-done(((f32[1024,2048]{1,0:T(8,128)}), f32[128,2048]{1,0:T(8,128)}) %reduce-scatter.7.cloned.1.call-update) | async-done | bytes 1048592 | tf_op jit(solution)/shard_map/reduce_scatter | solution.py:325
  631.7 6.4 convolution_convert_fusion
  643.9 29.3 %all-to-all-done.1 = bf16[8,128,256]{1,2,0:T(8,128)(2,1)S(1)} async-done(((bf16[8,128,256]{1,2,0:T(8,128)(2,1)}), bf16[8,128,256]{1,2,0:T(8,128)(2,1)S(1)}, u32[]{:S(2)}, u32[]{:S(2)}) %all-to-all-start.1) | async-done | bytes 524320 | tf_op jit(solution)/shard_map/all_to_all | solution.py:332
  673.5 18.2 %attend_back.1 = (f32[256,1024]{1,0:T(8,128)S(1)}, f32[2,4096,256]{2,1,0:T(8,128)}) custom-call(s32[2,4]{1,0:T(2,128)S(1)} %pad_add_fusion.bounds, bf16[1024,256]{1,0:T(8,128)(2,1)S(1)} %bitcast.94, bf16[4096,512]{1,0:T(8,128)(2,1)} %all-gather.9.cloned.1.call-done.key_ref.value_ref, bf16[512,4096]{1,0:T(8,128)(2,1)} %copy.85.value_t_ref.key_t_ref, ...), custom_call_target="tpu_custom_call" | custom-call | flops 15032385536 | bytes 16777216 | tf_op jit(solution)/shard_map/attend_back/pallas_call | solution.py:201
  699.0 7.1 collective-permute-done.8
  713.8 6.4 collective-permute-start.9
  722.9 43.8 %collective-permute-done.9 = f32[2,1024,256]{2,1,0:T(8,128)} collective-permute-done((f32[2,1024,256]{2,1,0:T(8,128)}, f32[2,1024,256]{2,1,0:T(8,128)}, u32[]{:S(2)}, u32[]{:S(2)}) %collective-permute-start.9) | collective-permute-done | bytes 2097184 | tf_op jit(solution)/shard_map/ppermute | solution.py:352
  792.9 149.6 %reduce-scatter.11.cloned.1.call-done = f32[128,2048]{1,0:T(8,128)} async-done(((f32[1024,2048]{1,0:T(8,128)}), f32[128,2048]{1,0:T(8,128)}) %reduce-scatter.11.cloned.1.call-update) | async-done | bytes 1048592 | tf_op jit(solution)/shard_map/reduce_scatter | solution.py:366
  966.2 6.2 fusion.61
  989.6 53.3 %collective-permute-done.29 = f32[344,2048]{1,0:T(8,128)} collective-permute-done((f32[344,2048]{1,0:T(8,128)S(1)}, f32[344,2048]{1,0:T(8,128)}, u32[]{:S(2)}, u32[]{:S(2)}) %collective-permute-start.29) | collective-permute-done | bytes 2818080 | tf_op jit(solution)/shard_map/ppermute | solution.py:257
  1045.1 58.0 %collective-permute-done.23 = f32[1024,688]{0,1:T(8,128)S(1)} collective-permute-done((f32[1024,688]{0,1:T(8,128)S(1)}, f32[1024,688]{0,1:T(8,128)S(1)}, u32[]{:S(2)}, u32[]{:S(2)}) %collective-permute-start.23) | collective-permute-done | bytes 2818080 | tf_op jit(solution)/shard_map/ppermute | solution.py:257
  1105.3 95.4 %all_gather.25 = s32[4096]{0:T(1024)S(1)} all-gather(s32[1024]{0:T(1024)S(1)} %copy-done.40), channel_id=1, replica_groups=mesh['tp'=8,'cp'=4] {'cp'}, dimensions={0}, use_global_device_ids=true | all-gather | bytes 20480 | tf_op jit(solution)/shard_map/all_gather | solution.py:303
  1211.3 6.5 broadcast_select_fusion.5
  1246.3 41.0 %collective-permute-done.11 = f32[1024,256]{1,0:T(8,128)S(1)} collective-permute-done((f32[1024,256]{1,0:T(8,128)S(1)}, f32[1024,256]{1,0:T(8,128)S(1)}, u32[]{:S(2)}, u32[]{:S(2)}) %collective-permute-start.11) | collective-permute-done | bytes 1048608 | tf_op jit(solution)/shard_map/ppermute | solution.py:257
  1290.5 36.3 %collective-permute-done.14 = f32[1024,256]{1,0:T(8,128)S(1)} collective-permute-done((f32[1024,256]{1,0:T(8,128)S(1)}, f32[1024,256]{1,0:T(8,128)S(1)}, u32[]{:S(2)}, u32[]{:S(2)}) %collective-permute-start.14) | collective-permute-done | bytes 1048608 | tf_op jit(solution)/shard_map/ppermute | solution.py:257
  1334.9 14.5 collective-permute-done.17
  1349.5 22.0 %collective-permute-done.20 = f32[128,2048]{1,0:T(8,128)S(1)} collective-permute-done((f32[128,2048]{1,0:T(8,128)S(1)}, f32[128,2048]{1,0:T(8,128)S(1)}, u32[]{:S(2)}, u32[]{:S(2)}) %collective-permute-start.20) | collective-permute-done | bytes 1048608 | tf_op jit(solution)/shard_map/ppermute | solution.py:257
  1378.4 39.4 %psum.7 = f32[2,2048]{1,0:T(2,128)S(1)} all-reduce(f32[2,2048]{1,0:T(2,128)S(1)} %pad_maximum_fusion.12), channel_id=1, replica_groups=mesh['tp'=8,'cp'=4] {'tp','cp'}, use_global_device_ids=true, to_apply=%region_13.15 | all-reduce | flops 4096 | bytes 32768 | tf_op jit(solution)/shard_map/psum | solution.py:376
  1418.4 65.8 %scatter_custom_fusion = f32[4032,2048]{1,0:T(8,128)} fusion(s32[4096]{0:T(1024)S(1)} %compare_select_fusion, f32[4096,2048]{1,0:T(8,128)} %all-gather.15.cloned.1.call-done, f32[]{:T(128)} %constant.160.clone.1), kind=kCustom, calls=%fused_computation.4 | custom fusion | flops 8388608 | bytes 33030656 | tf_op jit(solution)/shard_map/scatter-add | solution.py:375
  (310 shorter events, 275.8 us)
Async XLA Ops:
  7.2 113.6 %reduce-scatter.5.cloned.1.call-start = ((), (), s32[]{:S(2)}) async-start(), calls=%async_computation.6 | async-start | bytes 4718592 | tf_op jit(solution)/shard_map/reduce_scatter | solution.py:288
  29.5 167.1 %all-gather.7.cloned.1.call-start = ((), (), s32[]{:S(2)}) async-start(), calls=%async_computation.7 | async-start | bytes 4718592 | tf_op jit(solution)/shard_map/all_gather | solution.py:291
  124.0 172.6 %all-gather.9.cloned.1.call-start = ((), (), s32[]{:S(2)}) async-start(), calls=%async_computation.8 | async-start | bytes 5242880 | tf_op jit(solution)/shard_map/all_gather | solution.py:301
  228.6 58.5 %collective-permute-start.2 = (bf16[128,2048]{1,0:T(8,128)(2,1)S(1)}, bf16[128,2048]{1,0:T(8,128)(2,1)S(1)}, u32[]{:S(2)}, u32[]{:S(2)}) collective-permute-start(bf16[128,2048]{1,0:T(8,128)(2,1)S(1)} %get-tuple-element.31), channel_id=1, source_target_pairs={{0,12},{4,16},{8,20},{12,24},{16,28},{20,0},{24,4},{28,8},{1,13},{... | collective-permute-start | bytes 1572872 | tf_op jit(solution)/shard_map/ppermute | solution.py:269
  230.8 57.4 %collective-permute-start.3 = (bf16[128,2048]{1,0:T(8,128)(2,1)S(1)}, bf16[128,2048]{1,0:T(8,128)(2,1)S(1)}, u32[]{:S(2)}, u32[]{:S(2)}) collective-permute-start(bf16[128,2048]{1,0:T(8,128)(2,1)S(1)} %get-tuple-element.31), channel_id=1, source_target_pairs={{0,16},{4,20},{8,24},{12,28},{16,0},{20,4},{24,8},{28,12},{1,17},{... | collective-permute-start | bytes 1572872 | tf_op jit(solution)/shard_map/ppermute | solution.py:269
  233.4 55.9 %collective-permute-start.4 = (bf16[128,2048]{1,0:T(8,128)(2,1)S(1)}, bf16[128,2048]{1,0:T(8,128)(2,1)S(1)}, u32[]{:S(2)}, u32[]{:S(2)}) collective-permute-start(bf16[128,2048]{1,0:T(8,128)(2,1)S(1)} %get-tuple-element.31), channel_id=1, source_target_pairs={{0,20},{4,24},{8,28},{12,0},{16,4},{20,8},{24,12},{28,16},{1,21},{... | collective-permute-start | bytes 1572872 | tf_op jit(solution)/shard_map/ppermute | solution.py:269
  244.5 45.9 %collective-permute-start.5 = (bf16[128,2048]{1,0:T(8,128)(2,1)S(1)}, bf16[128,2048]{1,0:T(8,128)(2,1)S(1)}, u32[]{:S(2)}, u32[]{:S(2)}) collective-permute-start(bf16[128,2048]{1,0:T(8,128)(2,1)S(1)} %get-tuple-element.31), channel_id=1, source_target_pairs={{0,24},{4,28},{8,0},{12,4},{16,8},{20,12},{24,16},{28,20},{1,25},{... | collective-permute-start | bytes 1572872 | tf_op jit(solution)/shard_map/ppermute | solution.py:269
  245.6 48.4 %collective-permute-start.6 = (bf16[128,2048]{1,0:T(8,128)(2,1)S(1)}, bf16[128,2048]{1,0:T(8,128)(2,1)S(1)}, u32[]{:S(2)}, u32[]{:S(2)}) collective-permute-start(bf16[128,2048]{1,0:T(8,128)(2,1)S(1)} %get-tuple-element.31), channel_id=1, source_target_pairs={{0,28},{4,0},{8,4},{12,8},{16,12},{20,16},{24,20},{28,24},{1,29},{... | collective-permute-start | bytes 1572872 | tf_op jit(solution)/shard_map/ppermute | solution.py:269
  295.1 60.3 %collective-permute-start.7 = (bf16[1024,2048]{1,0:T(8,128)(2,1)}, bf16[1024,2048]{1,0:T(8,128)(2,1)}, u32[]{:S(2)}, u32[]{:S(2)}) collective-permute-start(bf16[1024,2048]{1,0:T(8,128)(2,1)} %get-tuple-element.68), channel_id=1, source_target_pairs={{0,1},{1,0},{2,3},{3,2},{4,5},{5,4},{6,7},{7,6},{8,9},{9,8},{10,11... | collective-permute-start | bytes 12582920 | tf_op jit(solution)/shard_map/ppermute | solution.py:271
  322.9 47.0 %all-to-all-start = ((bf16[8,128,256]{2,1,0:T(8,128)(2,1)}), bf16[8,128,256]{2,1,0:T(8,128)(2,1)}, u32[]{:S(2)}, u32[]{:S(2)}) async-start(bf16[8,128,256]{2,1,0:T(8,128)(2,1)} %bitcast.106), calls=%async_computation.1 | async-start | bytes 1048576 | tf_op jit(solution)/shard_map/all_to_all | solution.py:311
  355.3 106.1 %all-gather.11.cloned.1.call-start = ((), (), s32[]{:S(2)}) async-start(), calls=%async_computation.9 | async-start | bytes 4718592 | tf_op jit(solution)/shard_map/all_gather | solution.py:314
  386.3 242.0 %reduce-scatter.7.cloned.1.call-start = ((), (), s32[]{:S(2)}) async-start(), calls=%async_computation.10 | async-start | bytes 9437184 | tf_op jit(solution)/shard_map/reduce_scatter | solution.py:325
  482.2 309.5 %reduce-scatter.9.cloned.1.call-start = ((), (), s32[]{:S(2)}) async-start(), calls=%async_computation.11 | async-start | bytes 9437184 | tf_op jit(solution)/shard_map/reduce_scatter | solution.py:340
  640.2 33.1 %all-to-all-start.1 = ((bf16[8,128,256]{1,2,0:T(8,128)(2,1)}), bf16[8,128,256]{1,2,0:T(8,128)(2,1)S(1)}, u32[]{:S(2)}, u32[]{:S(2)}) async-start(bf16[8,128,256]{1,2,0:T(8,128)(2,1)} %broadcast_select_fusion.6), calls=%async_computation.3 | async-start | bytes 1048576 | tf_op jit(solution)/shard_map/all_to_all | solution.py:332
  643.9 298.6 %reduce-scatter.11.cloned.1.call-start = ((), (), s32[]{:S(2)}) async-start(), calls=%async_computation.13 | async-start | bytes 9437184 | tf_op jit(solution)/shard_map/reduce_scatter | solution.py:366
  713.8 52.9 %collective-permute-start.9 = (f32[2,1024,256]{2,1,0:T(8,128)}, f32[2,1024,256]{2,1,0:T(8,128)}, u32[]{:S(2)}, u32[]{:S(2)}) collective-permute-start(f32[2,1024,256]{2,1,0:T(8,128)} %dynamic-slice_bitcast_fusion.1), channel_id=1, source_target_pairs={{0,2},{1,3},{2,0},{3,1},{4,6},{5,7},{6,4},{7,5},{8,10},{9,11},{10,... | collective-permute-start | bytes 6291464 | tf_op jit(solution)/shard_map/ppermute | solution.py:352
  791.7 437.9 %all-gather.17.cloned.1.call-start = ((), (), s32[]{:S(2)}) async-start(), calls=%async_computation.15 | async-start | bytes 4718592 | tf_op jit(solution)/shard_map/all_gather | solution.py:341
  792.4 626.0 %all-gather.13.cloned.1.call-start = ((), (), s32[]{:S(2)}) async-start(), calls=%async_computation.12 | async-start | bytes 4718592 | tf_op jit(solution)/shard_map/all_gather | solution.py:369
  947.5 470.9 %all-gather.15.cloned.1.call-start = ((), (), s32[]{:S(2)}) async-start(), calls=%async_computation.14 | async-start | bytes 34603008 | tf_op jit(solution)/shard_map/all_gather | solution.py:372
  978.7 64.1 %collective-permute-start.29 = (f32[344,2048]{1,0:T(8,128)S(1)}, f32[344,2048]{1,0:T(8,128)}, u32[]{:S(2)}, u32[]{:S(2)}) collective-permute-start(f32[344,2048]{1,0:T(8,128)S(1)} %dynamic-slice_add_fusion), channel_id=1, source_target_pairs={{0,2},{1,3},{2,0},{3,1},{4,6},{5,7},{6,4},{7,5},{8,10},{9,11},{10,... | collective-permute-start | bytes 8454152 | tf_op jit(solution)/shard_map/ppermute | solution.py:257
  983.4 119.8 %collective-permute-start.23 = (f32[1024,688]{0,1:T(8,128)S(1)}, f32[1024,688]{0,1:T(8,128)S(1)}, u32[]{:S(2)}, u32[]{:S(2)}) collective-permute-start(f32[1024,688]{0,1:T(8,128)S(1)} %dynamic-slice_add_fusion.2), channel_id=1, source_target_pairs={{0,2},{1,3},{2,0},{3,1},{4,6},{5,7},{6,4},{7,5},{8,10},{9,11},{10,... | collective-permute-start | bytes 8454152 | tf_op jit(solution)/shard_map/ppermute | solution.py:257
  988.4 212.3 %collective-permute-start.26 = (f32[1024,688]{0,1:T(8,128)}, f32[1024,688]{0,1:T(8,128)}, u32[]{:S(2)}, u32[]{:S(2)}) collective-permute-start(f32[1024,688]{0,1:T(8,128)} %dynamic-slice_add_fusion.1), channel_id=1, source_target_pairs={{0,2},{1,3},{2,0},{3,1},{4,6},{5,7},{6,4},{7,5},{8,10},{9,11},{10,... | collective-permute-start | bytes 8454152 | tf_op jit(solution)/shard_map/ppermute | solution.py:257
  1045.0 161.0 %collective-permute-start.30 = (f32[344,2048]{1,0:T(8,128)S(1)}, f32[344,2048]{1,0:T(8,128)}, u32[]{:S(2)}, u32[]{:S(2)}) collective-permute-start(f32[344,2048]{1,0:T(8,128)S(1)} %add.325), channel_id=1, source_target_pairs={{0,1},{1,0},{2,3},{3,2},{4,5},{5,4},{6,7},{7,6},{8,9},{9,8},{10,11... | collective-permute-start | bytes 8454152 | tf_op jit(solution)/shard_map/ppermute | solution.py:259
  1105.3 106.0 %collective-permute-start.24 = (f32[1024,688]{0,1:T(8,128)}, f32[1024,688]{0,1:T(8,128)}, u32[]{:S(2)}, u32[]{:S(2)}) collective-permute-start(f32[1024,688]{0,1:T(8,128)} %add.319), channel_id=1, source_target_pairs={{0,1},{1,0},{2,3},{3,2},{4,5},{5,4},{6,7},{7,6},{8,9},{9,8},{10,11... | collective-permute-start | bytes 8454152 | tf_op jit(solution)/shard_map/ppermute | solution.py:259
  1205.7 27.9 %collective-permute-start.27 = (f32[1024,688]{0,1:T(8,128)}, f32[1024,688]{0,1:T(8,128)}, u32[]{:S(2)}, u32[]{:S(2)}) collective-permute-start(f32[1024,688]{0,1:T(8,128)} %add.321), channel_id=1, source_target_pairs={{0,1},{1,0},{2,3},{3,2},{4,5},{5,4},{6,7},{7,6},{8,9},{9,8},{10,11... | collective-permute-start | bytes 8454152 | tf_op jit(solution)/shard_map/ppermute | solution.py:259
  1238.7 48.6 %collective-permute-start.11 = (f32[1024,256]{1,0:T(8,128)S(1)}, f32[1024,256]{1,0:T(8,128)S(1)}, u32[]{:S(2)}, u32[]{:S(2)}) collective-permute-start(f32[1024,256]{1,0:T(8,128)S(1)} %dynamic-slice_add_fusion.6), channel_id=1, source_target_pairs={{0,2},{1,3},{2,0},{3,1},{4,6},{5,7},{6,4},{7,5},{8,10},{9,11},{10,... | collective-permute-start | bytes 3145736 | tf_op jit(solution)/shard_map/ppermute | solution.py:257
  1241.5 85.3 %collective-permute-start.14 = (f32[1024,256]{1,0:T(8,128)S(1)}, f32[1024,256]{1,0:T(8,128)S(1)}, u32[]{:S(2)}, u32[]{:S(2)}) collective-permute-start(f32[1024,256]{1,0:T(8,128)S(1)} %dynamic-slice_add_fusion.5), channel_id=1, source_target_pairs={{0,2},{1,3},{2,0},{3,1},{4,6},{5,7},{6,4},{7,5},{8,10},{9,11},{10,... | collective-permute-start | bytes 3145736 | tf_op jit(solution)/shard_map/ppermute | solution.py:257
  1244.0 105.3 %collective-permute-start.17 = (f32[1024,256]{1,0:T(8,128)S(1)}, f32[1024,256]{1,0:T(8,128)S(1)}, u32[]{:S(2)}, u32[]{:S(2)}) collective-permute-start(f32[1024,256]{1,0:T(8,128)S(1)} %dynamic-slice_add_fusion.4), channel_id=1, source_target_pairs={{0,2},{1,3},{2,0},{3,1},{4,6},{5,7},{6,4},{7,5},{8,10},{9,11},{10,... | collective-permute-start | bytes 3145736 | tf_op jit(solution)/shard_map/ppermute | solution.py:257
  1245.4 126.1 %collective-permute-start.20 = (f32[128,2048]{1,0:T(8,128)S(1)}, f32[128,2048]{1,0:T(8,128)S(1)}, u32[]{:S(2)}, u32[]{:S(2)}) collective-permute-start(f32[128,2048]{1,0:T(8,128)S(1)} %dynamic-slice_add_fusion.3), channel_id=1, source_target_pairs={{0,2},{1,3},{2,0},{3,1},{4,6},{5,7},{6,4},{7,5},{8,10},{9,11},{10,... | collective-permute-start | bytes 3145736 | tf_op jit(solution)/shard_map/ppermute | solution.py:257
  1287.4 84.3 %collective-permute-start.12 = (f32[1024,256]{1,0:T(8,128)S(1)}, f32[1024,256]{1,0:T(8,128)S(1)}, u32[]{:S(2)}, u32[]{:S(2)}) collective-permute-start(f32[1024,256]{1,0:T(8,128)S(1)} %add.310), channel_id=1, source_target_pairs={{0,1},{1,0},{2,3},{3,2},{4,5},{5,4},{6,7},{7,6},{8,9},{9,8},{10,11... | collective-permute-start | bytes 3145736 | tf_op jit(solution)/shard_map/ppermute | solution.py:259
  1327.0 44.9 %collective-permute-start.15 = (f32[1024,256]{1,0:T(8,128)S(1)}, f32[1024,256]{1,0:T(8,128)S(1)}, u32[]{:S(2)}, u32[]{:S(2)}) collective-permute-start(f32[1024,256]{1,0:T(8,128)S(1)} %add.312), channel_id=1, source_target_pairs={{0,1},{1,0},{2,3},{3,2},{4,5},{5,4},{6,7},{7,6},{8,9},{9,8},{10,11... | collective-permute-start | bytes 3145736 | tf_op jit(solution)/shard_map/ppermute | solution.py:259
  1349.5 25.7 %collective-permute-start.18 = (f32[1024,256]{1,0:T(8,128)S(1)}, f32[1024,256]{1,0:T(8,128)S(1)}, u32[]{:S(2)}, u32[]{:S(2)}) collective-permute-start(f32[1024,256]{1,0:T(8,128)S(1)} %add.314), channel_id=1, source_target_pairs={{0,1},{1,0},{2,3},{3,2},{4,5},{5,4},{6,7},{7,6},{8,9},{9,8},{10,11... | collective-permute-start | bytes 3145736 | tf_op jit(solution)/shard_map/ppermute | solution.py:259
  (64 other events, 1845.7 us)
Sparse Core Ops, SparseCore 0:
  29.7 91.0 reduce-scatter.4
  124.2 72.3 all-gather.6
  225.0 32.9 all-gather.8
  386.5 74.8 all-gather.10
  482.3 145.9 reduce-scatter.6
  631.8 159.7 reduce-scatter.8
  795.9 146.5 reduce-scatter.10
  944.6 71.8 all-gather.16
  1018.7 71.3 all-gather.12
  1092.9 266.5 all-gather.14

commit v3 on v2

--- a/solution.py
+++ b/solution.py
@@ -292,12 +292,20 @@
         angle = pos.astype(jnp.float32)[:, None, None] * inv_freq
         cosine = jnp.cos(angle)
         sine = jnp.sin(angle)
-        query = jnp.dot(act_a, w_q, preferred_element_type=jnp.float32).reshape(span, heads, head_dim)
-        query = rotate(query, cosine, sine).astype(jnp.bfloat16).reshape(span, local_dim)
-        key_loc = jnp.dot(act_a, w_k, preferred_element_type=jnp.float32).reshape(span, heads, head_dim)
-        key_loc = rotate(key_loc, cosine, sine).astype(jnp.bfloat16)
+        cos_row = jnp.tile(cosine[:, 0], (1, 2 * heads))
+        sin_row = jnp.tile(sine[:, 0], (1, 2 * heads))
+
+        def project(weight):
+            pairs = weight.reshape(width, heads, 2, head_dim // 2)
+            turned = jnp.stack([-pairs[:, :, 1], pairs[:, :, 0]], axis=2).reshape(width, local_dim)
+            straight = jnp.dot(act_a, weight, preferred_element_type=jnp.float32)
+            crossed = jnp.dot(act_a, turned, preferred_element_type=jnp.float32)
+            return (straight * cos_row + crossed * sin_row).astype(jnp.bfloat16)
+
+        query = project(w_q)
+        key_loc = project(w_k)
         value_loc = jnp.dot(act_a, w_v, preferred_element_type=jnp.float32).astype(jnp.bfloat16)
-        key_value = jnp.concatenate([key_loc.reshape(span, local_dim), value_loc], axis=1)
+        key_value = jnp.concatenate([key_loc, value_loc], axis=1)
         kv_all = lax.all_gather(key_value, "cp", axis=0, tiled=True)
         kv_all_t = kv_all.T
         token_all = lax.all_gather(tokens, "cp", axis=0, tiled=True)

time: 1500 us -> 1490 us (level)
    unnamed x123 -> x131, local copies, waits for them, and re-layouts: 48.6 us -> 41.9 us
  transfers between devices with their start and end apart: 43 -> 43, of which waited for: 19 -> 19; matrix products, arithmetic and copies ran while one was open for 12% -> 13% of each run, Pallas kernels for 2% -> 2%
where the time goes in v3:
time: 1490 us; the launch traced here: 1480 us
  waiting for transfers between devices  869 us (58%)
  other arithmetic  165 us (11%)
  blocking collectives  135 us (9%)
  local copies, waits for them, and re-layouts  108 us (7%)
  matrix products  89.3 us (6%)
  starting transfers between devices  73.2 us (5%)
  Pallas kernels  29.9 us (2%)
  between operations  15.5 us (1%)
    ppermute x7, waiting for transfers between devices, cp_sum(): far_part = lax.ppermute(chip_half, 'cp', chip_swap)  225 us
    reduce_scatter x1, waiting for transfers between devices, device_step(): d_act_a = lax.psum_scatter(d_act_a, 'tp', scatter_dimension=0, tiled=True)  150 us
    reduce_scatter x1, waiting for transfers between devices, device_step(): d_act_b = lax.psum_scatter(d_act_b, 'tp', scatter_dimension=0, tiled=True)  137 us
    all_gather x1, blocking collectives, device_step(): token_all = lax.all_gather(tokens, 'cp', axis=0, tiled=True)  95.4 us
    reduce_scatter x1, waiting for transfers between devices, device_step(): lax.psum_scatter(picked, 'tp', scatter_dimension=0, tiled=True)  90.5 us
    all_gather x1, waiting for transfers between devices, device_step(): lax.all_gather((normed_b * gain_b).astype(jnp.bfloat16), 'tp', axis=0, ti...  67.6 us
    scatter-add x1, other arithmetic, device_step(): jnp.zeros((rows, width), jnp.float32).at[drop_ids]  65.8 us
    all_gather x1, waiting for transfers between devices, device_step(): lax.all_gather((normed_a * gain_a).astype(jnp.bfloat16), 'tp', axis=0, ti...  58.8 us
  transfers between devices with their start and end apart: 43, of which 19 were waited for; matrix products, arithmetic and copies ran while one was open for 13% of the time, Pallas kernels for 2%

profile of v3, /device:TPU:0, one launch (start us, length us, event | category | flops | bytes accessed | tf_op | source)
XLA Modules:
  0.0 1484.3 jit_solution(7858032374421693493)
XLA Ops:
  8.8 16.6 %gather_fusion = bf16[1024,2048]{1,0:T(8,128)(2,1)} fusion(bf16[4032,2048]{1,0:T(8,128)(2,1)} %param.20, s32[1024]{0:T(1024)S(1)} %fusion.50), kind=kCustom, calls=%fused_computation.2 | custom fusion | bytes 8392704 | tf_op jit(solution)/shard_map/jit(_take)/gather | solution.py:287
  30.2 90.5 %reduce-scatter.5.cloned.1.call-done = bf16[128,2048]{1,0:T(8,128)(2,1)} async-done(((bf16[1024,2048]{1,0:T(8,128)(2,1)}), bf16[128,2048]{1,0:T(8,128)(2,1)}) %reduce-scatter.5.cloned.1.call-update) | async-done | bytes 524304 | tf_op jit(solution)/shard_map/reduce_scatter | solution.py:288
  137.8 58.8 %all-gather.7.cloned.1.call-done = bf16[1024,2048]{1,0:T(8,128)(2,1)} async-done(((bf16[128,2048]{1,0:T(8,128)(2,1)}), bf16[1024,2048]{1,0:T(8,128)(2,1)}) %all-gather.7.cloned.1.call-update) | async-done | bytes 4194320 | tf_op jit(solution)/shard_map/all_gather | solution.py:291
  214.5 10.0 collective-permute-done
  225.6 10.1 collective-permute-start.6
  236.8 30.3 %collective-permute-done.2 = bf16[128,2048]{1,0:T(8,128)(2,1)S(1)} collective-permute-done((bf16[128,2048]{1,0:T(8,128)(2,1)S(1)}, bf16[128,2048]{1,0:T(8,128)(2,1)S(1)}, u32[]{:S(2)}, u32[]{:S(2)}) %collective-permute-start.2) | collective-permute-done | bytes 524320 | tf_op jit(solution)/shard_map/ppermute | solution.py:269
  284.6 6.3 copy.105.value_t_ref.key_t_ref
  295.3 11.7 attend.1
  310.9 32.4 %all-to-all-start = ((bf16[8,128,256]{2,1,0:T(8,128)(2,1)}), bf16[8,128,256]{2,1,0:T(8,128)(2,1)}, u32[]{:S(2)}, u32[]{:S(2)}) async-start(bf16[8,128,256]{2,1,0:T(8,128)(2,1)} %bitcast.104), calls=%async_computation.1 | async-start | bytes 1048576 | tf_op jit(solution)/shard_map/all_to_all | solution.py:319
  348.2 9.7 all-to-all-done
  374.5 7.3 convolution_convert_fusion.1
  381.8 67.6 %all-gather.11.cloned.1.call-done = bf16[1024,2048]{1,0:T(8,128)(2,1)} async-done(((bf16[128,2048]{1,0:T(8,128)(2,1)}), bf16[1024,2048]{1,0:T(8,128)(2,1)}) %all-gather.11.cloned.1.call-update) | async-done | bytes 4194320 | tf_op jit(solution)/shard_map/all_gather | solution.py:322
  471.9 7.1 fusion.62
  479.0 137.2 %reduce-scatter.7.cloned.1.call-done = f32[128,2048]{1,0:T(8,128)} async-done(((f32[1024,2048]{1,0:T(8,128)}), f32[128,2048]{1,0:T(8,128)}) %reduce-scatter.7.cloned.1.call-update) | async-done | bytes 1048592 | tf_op jit(solution)/shard_map/reduce_scatter | solution.py:333
  619.6 6.5 convolution_convert_fusion
  631.9 29.3 %all-to-all-done.1 = bf16[8,128,256]{1,2,0:T(8,128)(2,1)S(1)} async-done(((bf16[8,128,256]{1,2,0:T(8,128)(2,1)}), bf16[8,128,256]{1,2,0:T(8,128)(2,1)S(1)}, u32[]{:S(2)}, u32[]{:S(2)}) %all-to-all-start.1) | async-done | bytes 524320 | tf_op jit(solution)/shard_map/all_to_all | solution.py:340
  661.4 18.2 %attend_back.1 = (f32[256,1024]{1,0:T(8,128)S(1)}, f32[2,4096,256]{2,1,0:T(8,128)}) custom-call(s32[2,4]{1,0:T(2,128)S(1)} %pad_add_fusion.bounds, bf16[1024,256]{1,0:T(8,128)(2,1)S(1)} %fusion.15.query_ref, bf16[4096,512]{1,0:T(8,128)(2,1)} %all-gather.9.cloned.1.call-done.key_ref.value_ref, bf16[512,4096]{1,0:T(8,128)(2,1)} %copy.105.value_t_ref.key_t_ref, ...), custom_call_target="tpu_custom_call" | custom-call | flops 15032385536 | bytes 16777216 | tf_op jit(solution)/shard_map/attend_back/pallas_call | solution.py:201
  690.8 7.1 collective-permute-done.8
  705.4 6.1 collective-permute-start.9
  712.7 45.4 %collective-permute-done.9 = f32[2,1024,256]{2,1,0:T(8,128)} collective-permute-done((f32[2,1024,256]{2,1,0:T(8,128)}, f32[2,1024,256]{2,1,0:T(8,128)}, u32[]{:S(2)}, u32[]{:S(2)}) %collective-permute-start.9) | collective-permute-done | bytes 2097184 | tf_op jit(solution)/shard_map/ppermute | solution.py:360
  780.4 150.0 %reduce-scatter.11.cloned.1.call-done = f32[128,2048]{1,0:T(8,128)} async-done(((f32[1024,2048]{1,0:T(8,128)}), f32[128,2048]{1,0:T(8,128)}) %reduce-scatter.11.cloned.1.call-update) | async-done | bytes 1048592 | tf_op jit(solution)/shard_map/reduce_scatter | solution.py:374
  954.1 6.2 fusion.53
  977.5 53.3 %collective-permute-done.29 = f32[344,2048]{1,0:T(8,128)} collective-permute-done((f32[344,2048]{1,0:T(8,128)S(1)}, f32[344,2048]{1,0:T(8,128)}, u32[]{:S(2)}, u32[]{:S(2)}) %collective-permute-start.29) | collective-permute-done | bytes 2818080 | tf_op jit(solution)/shard_map/ppermute | solution.py:257
  1033.0 58.0 %collective-permute-done.23 = f32[1024,688]{0,1:T(8,128)S(1)} collective-permute-done((f32[1024,688]{0,1:T(8,128)S(1)}, f32[1024,688]{0,1:T(8,128)S(1)}, u32[]{:S(2)}, u32[]{:S(2)}) %collective-permute-start.23) | collective-permute-done | bytes 2818080 | tf_op jit(solution)/shard_map/ppermute | solution.py:257
  1093.2 95.4 %all_gather.25 = s32[4096]{0:T(1024)S(1)} all-gather(s32[1024]{0:T(1024)S(1)} %copy-done.46), channel_id=1, replica_groups=mesh['tp'=8,'cp'=4] {'cp'}, dimensions={0}, use_global_device_ids=true | all-gather | bytes 20480 | tf_op jit(solution)/shard_map/all_gather | solution.py:311
  1199.2 6.5 broadcast_select_fusion.5
  1234.2 41.0 %collective-permute-done.11 = f32[1024,256]{1,0:T(8,128)S(1)} collective-permute-done((f32[1024,256]{1,0:T(8,128)S(1)}, f32[1024,256]{1,0:T(8,128)S(1)}, u32[]{:S(2)}, u32[]{:S(2)}) %collective-permute-start.11) | collective-permute-done | bytes 1048608 | tf_op jit(solution)/shard_map/ppermute | solution.py:257
  1278.4 36.3 %collective-permute-done.14 = f32[1024,256]{1,0:T(8,128)S(1)} collective-permute-done((f32[1024,256]{1,0:T(8,128)S(1)}, f32[1024,256]{1,0:T(8,128)S(1)}, u32[]{:S(2)}, u32[]{:S(2)}) %collective-permute-start.14) | collective-permute-done | bytes 1048608 | tf_op jit(solution)/shard_map/ppermute | solution.py:257
  1322.8 14.5 collective-permute-done.17
  1337.5 22.0 %collective-permute-done.20 = f32[128,2048]{1,0:T(8,128)S(1)} collective-permute-done((f32[128,2048]{1,0:T(8,128)S(1)}, f32[128,2048]{1,0:T(8,128)S(1)}, u32[]{:S(2)}, u32[]{:S(2)}) %collective-permute-start.20) | collective-permute-done | bytes 1048608 | tf_op jit(solution)/shard_map/ppermute | solution.py:257
  1366.4 39.4 %psum.7 = f32[2,2048]{1,0:T(2,128)S(1)} all-reduce(f32[2,2048]{1,0:T(2,128)S(1)} %pad_maximum_fusion.12), channel_id=1, replica_groups=mesh['tp'=8,'cp'=4] {'tp','cp'}, use_global_device_ids=true, to_apply=%region_13.15 | all-reduce | flops 4096 | bytes 32768 | tf_op jit(solution)/shard_map/psum | solution.py:384
  1406.4 65.8 %scatter_custom_fusion = f32[4032,2048]{1,0:T(8,128)} fusion(s32[4096]{0:T(1024)S(1)} %compare_select_fusion, f32[4096,2048]{1,0:T(8,128)} %all-gather.15.cloned.1.call-done, f32[]{:T(128)} %constant.160.clone.1), kind=kCustom, calls=%fused_computation.4 | custom fusion | flops 8388608 | bytes 33030656 | tf_op jit(solution)/shard_map/scatter-add | solution.py:383
  (323 shorter events, 272.2 us)
Async XLA Ops:
  7.2 113.6 %reduce-scatter.5.cloned.1.call-start = ((), (), s32[]{:S(2)}) async-start(), calls=%async_computation.6 | async-start | bytes 4718592 | tf_op jit(solution)/shard_map/reduce_scatter | solution.py:288
  29.5 167.1 %all-gather.7.cloned.1.call-start = ((), (), s32[]{:S(2)}) async-start(), calls=%async_computation.7 | async-start | bytes 4718592 | tf_op jit(solution)/shard_map/all_gather | solution.py:291
  124.0 160.5 %all-gather.9.cloned.1.call-start = ((), (), s32[]{:S(2)}) async-start(), calls=%async_computation.8 | async-start | bytes 5242880 | tf_op jit(solution)/shard_map/all_gather | solution.py:309
  208.6 58.5 %collective-permute-start.2 = (bf16[128,2048]{1,0:T(8,128)(2,1)S(1)}, bf16[128,2048]{1,0:T(8,128)(2,1)S(1)}, u32[]{:S(2)}, u32[]{:S(2)}) collective-permute-start(bf16[128,2048]{1,0:T(8,128)(2,1)S(1)} %get-tuple-element.31), channel_id=1, source_target_pairs={{0,12},{4,16},{8,20},{12,24},{16,28},{20,0},{24,4},{28,8},{1,13},{... | collective-permute-start | bytes 1572872 | tf_op jit(solution)/shard_map/ppermute | solution.py:269
  210.8 57.4 %collective-permute-start.3 = (bf16[128,2048]{1,0:T(8,128)(2,1)S(1)}, bf16[128,2048]{1,0:T(8,128)(2,1)S(1)}, u32[]{:S(2)}, u32[]{:S(2)}) collective-permute-start(bf16[128,2048]{1,0:T(8,128)(2,1)S(1)} %get-tuple-element.31), channel_id=1, source_target_pairs={{0,16},{4,20},{8,24},{12,28},{16,0},{20,4},{24,8},{28,12},{1,17},{... | collective-permute-start | bytes 1572872 | tf_op jit(solution)/shard_map/ppermute | solution.py:269
  213.3 55.9 %collective-permute-start.4 = (bf16[128,2048]{1,0:T(8,128)(2,1)S(1)}, bf16[128,2048]{1,0:T(8,128)(2,1)S(1)}, u32[]{:S(2)}, u32[]{:S(2)}) collective-permute-start(bf16[128,2048]{1,0:T(8,128)(2,1)S(1)} %get-tuple-element.31), channel_id=1, source_target_pairs={{0,20},{4,24},{8,28},{12,0},{16,4},{20,8},{24,12},{28,16},{1,21},{... | collective-permute-start | bytes 1572872 | tf_op jit(solution)/shard_map/ppermute | solution.py:269
  224.5 45.9 %collective-permute-start.5 = (bf16[128,2048]{1,0:T(8,128)(2,1)S(1)}, bf16[128,2048]{1,0:T(8,128)(2,1)S(1)}, u32[]{:S(2)}, u32[]{:S(2)}) collective-permute-start(bf16[128,2048]{1,0:T(8,128)(2,1)S(1)} %get-tuple-element.31), channel_id=1, source_target_pairs={{0,24},{4,28},{8,0},{12,4},{16,8},{20,12},{24,16},{28,20},{1,25},{... | collective-permute-start | bytes 1572872 | tf_op jit(solution)/shard_map/ppermute | solution.py:269
  225.6 48.4 %collective-permute-start.6 = (bf16[128,2048]{1,0:T(8,128)(2,1)S(1)}, bf16[128,2048]{1,0:T(8,128)(2,1)S(1)}, u32[]{:S(2)}, u32[]{:S(2)}) collective-permute-start(bf16[128,2048]{1,0:T(8,128)(2,1)S(1)} %get-tuple-element.31), channel_id=1, source_target_pairs={{0,28},{4,0},{8,4},{12,8},{16,12},{20,16},{24,20},{28,24},{1,29},{... | collective-permute-start | bytes 1572872 | tf_op jit(solution)/shard_map/ppermute | solution.py:269
  275.1 68.3 %collective-permute-start.7 = (bf16[1024,2048]{1,0:T(8,128)(2,1)}, bf16[1024,2048]{1,0:T(8,128)(2,1)}, u32[]{:S(2)}, u32[]{:S(2)}) collective-permute-start(bf16[1024,2048]{1,0:T(8,128)(2,1)} %get-tuple-element.62), channel_id=1, source_target_pairs={{0,1},{1,0},{2,3},{3,2},{4,5},{5,4},{6,7},{7,6},{8,9},{9,8},{10,11... | collective-permute-start | bytes 12582920 | tf_op jit(solution)/shard_map/ppermute | solution.py:271
  310.9 47.0 %all-to-all-start = ((bf16[8,128,256]{2,1,0:T(8,128)(2,1)}), bf16[8,128,256]{2,1,0:T(8,128)(2,1)}, u32[]{:S(2)}, u32[]{:S(2)}) async-start(bf16[8,128,256]{2,1,0:T(8,128)(2,1)} %bitcast.104), calls=%async_computation.1 | async-start | bytes 1048576 | tf_op jit(solution)/shard_map/all_to_all | solution.py:319
  343.3 106.1 %all-gather.11.cloned.1.call-start = ((), (), s32[]{:S(2)}) async-start(), calls=%async_computation.9 | async-start | bytes 4718592 | tf_op jit(solution)/shard_map/all_gather | solution.py:322
  374.3 242.0 %reduce-scatter.7.cloned.1.call-start = ((), (), s32[]{:S(2)}) async-start(), calls=%async_computation.10 | async-start | bytes 9437184 | tf_op jit(solution)/shard_map/reduce_scatter | solution.py:333
  470.1 309.4 %reduce-scatter.9.cloned.1.call-start = ((), (), s32[]{:S(2)}) async-start(), calls=%async_computation.11 | async-start | bytes 9437184 | tf_op jit(solution)/shard_map/reduce_scatter | solution.py:348
  628.1 33.1 %all-to-all-start.1 = ((bf16[8,128,256]{1,2,0:T(8,128)(2,1)}), bf16[8,128,256]{1,2,0:T(8,128)(2,1)S(1)}, u32[]{:S(2)}, u32[]{:S(2)}) async-start(bf16[8,128,256]{1,2,0:T(8,128)(2,1)} %broadcast_select_fusion.6), calls=%async_computation.3 | async-start | bytes 1048576 | tf_op jit(solution)/shard_map/all_to_all | solution.py:340
  631.8 298.6 %reduce-scatter.11.cloned.1.call-start = ((), (), s32[]{:S(2)}) async-start(), calls=%async_computation.13 | async-start | bytes 9437184 | tf_op jit(solution)/shard_map/reduce_scatter | solution.py:374
  705.4 52.6 %collective-permute-start.9 = (f32[2,1024,256]{2,1,0:T(8,128)}, f32[2,1024,256]{2,1,0:T(8,128)}, u32[]{:S(2)}, u32[]{:S(2)}) collective-permute-start(f32[2,1024,256]{2,1,0:T(8,128)} %dynamic-slice_bitcast_fusion), channel_id=1, source_target_pairs={{0,2},{1,3},{2,0},{3,1},{4,6},{5,7},{6,4},{7,5},{8,10},{9,11},{10,... | collective-permute-start | bytes 6291464 | tf_op jit(solution)/shard_map/ppermute | solution.py:360
  779.6 437.9 %all-gather.17.cloned.1.call-start = ((), (), s32[]{:S(2)}) async-start(), calls=%async_computation.15 | async-start | bytes 4718592 | tf_op jit(solution)/shard_map/all_gather | solution.py:349
  780.4 626.0 %all-gather.13.cloned.1.call-start = ((), (), s32[]{:S(2)}) async-start(), calls=%async_computation.12 | async-start | bytes 4718592 | tf_op jit(solution)/shard_map/all_gather | solution.py:377
  935.4 471.0 %all-gather.15.cloned.1.call-start = ((), (), s32[]{:S(2)}) async-start(), calls=%async_computation.14 | async-start | bytes 34603008 | tf_op jit(solution)/shard_map/all_gather | solution.py:380
  966.6 64.1 %collective-permute-start.29 = (f32[344,2048]{1,0:T(8,128)S(1)}, f32[344,2048]{1,0:T(8,128)}, u32[]{:S(2)}, u32[]{:S(2)}) collective-permute-start(f32[344,2048]{1,0:T(8,128)S(1)} %dynamic-slice_add_fusion), channel_id=1, source_target_pairs={{0,2},{1,3},{2,0},{3,1},{4,6},{5,7},{6,4},{7,5},{8,10},{9,11},{10,... | collective-permute-start | bytes 8454152 | tf_op jit(solution)/shard_map/ppermute | solution.py:257
  971.3 119.8 %collective-permute-start.23 = (f32[1024,688]{0,1:T(8,128)S(1)}, f32[1024,688]{0,1:T(8,128)S(1)}, u32[]{:S(2)}, u32[]{:S(2)}) collective-permute-start(f32[1024,688]{0,1:T(8,128)S(1)} %dynamic-slice_add_fusion.2), channel_id=1, source_target_pairs={{0,2},{1,3},{2,0},{3,1},{4,6},{5,7},{6,4},{7,5},{8,10},{9,11},{10,... | collective-permute-start | bytes 8454152 | tf_op jit(solution)/shard_map/ppermute | solution.py:257
  976.3 212.3 %collective-permute-start.26 = (f32[1024,688]{0,1:T(8,128)}, f32[1024,688]{0,1:T(8,128)}, u32[]{:S(2)}, u32[]{:S(2)}) collective-permute-start(f32[1024,688]{0,1:T(8,128)} %dynamic-slice_add_fusion.1), channel_id=1, source_target_pairs={{0,2},{1,3},{2,0},{3,1},{4,6},{5,7},{6,4},{7,5},{8,10},{9,11},{10,... | collective-permute-start | bytes 8454152 | tf_op jit(solution)/shard_map/ppermute | solution.py:257
  1033.0 161.0 %collective-permute-start.30 = (f32[344,2048]{1,0:T(8,128)S(1)}, f32[344,2048]{1,0:T(8,128)}, u32[]{:S(2)}, u32[]{:S(2)}) collective-permute-start(f32[344,2048]{1,0:T(8,128)S(1)} %add.325), channel_id=1, source_target_pairs={{0,1},{1,0},{2,3},{3,2},{4,5},{5,4},{6,7},{7,6},{8,9},{9,8},{10,11... | collective-permute-start | bytes 8454152 | tf_op jit(solution)/shard_map/ppermute | solution.py:259
  1093.2 106.0 %collective-permute-start.24 = (f32[1024,688]{0,1:T(8,128)}, f32[1024,688]{0,1:T(8,128)}, u32[]{:S(2)}, u32[]{:S(2)}) collective-permute-start(f32[1024,688]{0,1:T(8,128)} %add.319), channel_id=1, source_target_pairs={{0,1},{1,0},{2,3},{3,2},{4,5},{5,4},{6,7},{7,6},{8,9},{9,8},{10,11... | collective-permute-start | bytes 8454152 | tf_op jit(solution)/shard_map/ppermute | solution.py:259
  1193.6 27.9 %collective-permute-start.27 = (f32[1024,688]{0,1:T(8,128)}, f32[1024,688]{0,1:T(8,128)}, u32[]{:S(2)}, u32[]{:S(2)}) collective-permute-start(f32[1024,688]{0,1:T(8,128)} %add.321), channel_id=1, source_target_pairs={{0,1},{1,0},{2,3},{3,2},{4,5},{5,4},{6,7},{7,6},{8,9},{9,8},{10,11... | collective-permute-start | bytes 8454152 | tf_op jit(solution)/shard_map/ppermute | solution.py:259
  1226.6 48.6 %collective-permute-start.11 = (f32[1024,256]{1,0:T(8,128)S(1)}, f32[1024,256]{1,0:T(8,128)S(1)}, u32[]{:S(2)}, u32[]{:S(2)}) collective-permute-start(f32[1024,256]{1,0:T(8,128)S(1)} %dynamic-slice_add_fusion.6), channel_id=1, source_target_pairs={{0,2},{1,3},{2,0},{3,1},{4,6},{5,7},{6,4},{7,5},{8,10},{9,11},{10,... | collective-permute-start | bytes 3145736 | tf_op jit(solution)/shard_map/ppermute | solution.py:257
  1229.5 85.3 %collective-permute-start.14 = (f32[1024,256]{1,0:T(8,128)S(1)}, f32[1024,256]{1,0:T(8,128)S(1)}, u32[]{:S(2)}, u32[]{:S(2)}) collective-permute-start(f32[1024,256]{1,0:T(8,128)S(1)} %dynamic-slice_add_fusion.5), channel_id=1, source_target_pairs={{0,2},{1,3},{2,0},{3,1},{4,6},{5,7},{6,4},{7,5},{8,10},{9,11},{10,... | collective-permute-start | bytes 3145736 | tf_op jit(solution)/shard_map/ppermute | solution.py:257
  1231.9 105.3 %collective-permute-start.17 = (f32[1024,256]{1,0:T(8,128)S(1)}, f32[1024,256]{1,0:T(8,128)S(1)}, u32[]{:S(2)}, u32[]{:S(2)}) collective-permute-start(f32[1024,256]{1,0:T(8,128)S(1)} %dynamic-slice_add_fusion.4), channel_id=1, source_target_pairs={{0,2},{1,3},{2,0},{3,1},{4,6},{5,7},{6,4},{7,5},{8,10},{9,11},{10,... | collective-permute-start | bytes 3145736 | tf_op jit(solution)/shard_map/ppermute | solution.py:257
  1233.4 126.1 %collective-permute-start.20 = (f32[128,2048]{1,0:T(8,128)S(1)}, f32[128,2048]{1,0:T(8,128)S(1)}, u32[]{:S(2)}, u32[]{:S(2)}) collective-permute-start(f32[128,2048]{1,0:T(8,128)S(1)} %dynamic-slice_add_fusion.3), channel_id=1, source_target_pairs={{0,2},{1,3},{2,0},{3,1},{4,6},{5,7},{6,4},{7,5},{8,10},{9,11},{10,... | collective-permute-start | bytes 3145736 | tf_op jit(solution)/shard_map/ppermute | solution.py:257
  1275.3 84.3 %collective-permute-start.12 = (f32[1024,256]{1,0:T(8,128)S(1)}, f32[1024,256]{1,0:T(8,128)S(1)}, u32[]{:S(2)}, u32[]{:S(2)}) collective-permute-start(f32[1024,256]{1,0:T(8,128)S(1)} %add.310), channel_id=1, source_target_pairs={{0,1},{1,0},{2,3},{3,2},{4,5},{5,4},{6,7},{7,6},{8,9},{9,8},{10,11... | collective-permute-start | bytes 3145736 | tf_op jit(solution)/shard_map/ppermute | solution.py:259
  1314.9 44.9 %collective-permute-start.15 = (f32[1024,256]{1,0:T(8,128)S(1)}, f32[1024,256]{1,0:T(8,128)S(1)}, u32[]{:S(2)}, u32[]{:S(2)}) collective-permute-start(f32[1024,256]{1,0:T(8,128)S(1)} %add.312), channel_id=1, source_target_pairs={{0,1},{1,0},{2,3},{3,2},{4,5},{5,4},{6,7},{7,6},{8,9},{9,8},{10,11... | collective-permute-start | bytes 3145736 | tf_op jit(solution)/shard_map/ppermute | solution.py:259
  1337.4 25.7 %collective-permute-start.18 = (f32[1024,256]{1,0:T(8,128)S(1)}, f32[1024,256]{1,0:T(8,128)S(1)}, u32[]{:S(2)}, u32[]{:S(2)}) collective-permute-start(f32[1024,256]{1,0:T(8,128)S(1)} %add.314), channel_id=1, source_target_pairs={{0,1},{1,0},{2,3},{3,2},{4,5},{5,4},{6,7},{7,6},{8,9},{9,8},{10,11... | collective-permute-start | bytes 3145736 | tf_op jit(solution)/shard_map/ppermute | solution.py:259
  (71 other events, 1770.8 us)
Sparse Core Ops, SparseCore 0:
  29.7 91.0 reduce-scatter.4
  124.2 72.3 all-gather.6
  205.0 32.9 all-gather.8
  374.4 74.8 all-gather.10
  470.3 145.9 reduce-scatter.6
  619.8 159.7 reduce-scatter.8
  783.8 146.5 reduce-scatter.10
  932.5 71.9 all-gather.16
  1006.6 71.3 all-gather.12
  1080.8 266.5 all-gather.14
